TPU v7x, 256 devices: a whole 4x4x8 slice. The times are simulated.
256 devices in a mesh: seq: 32 (over y, z), grp: 8 (over x, core).
Axes of the slice: x: 4, y: 4, z: 8, core: 2. Of those that a mesh axis runs over, the one named last changes fastest.
Arguments:
- event_codes: int32 [2097152], P(('seq', 'grp')), may hold values from 0 to 255
- window_ends: int32 [196608], P(('seq', 'grp')), may hold values from 0 to 8191, as said below
- window_count: int32 [256], P(('seq', 'grp')), may hold values from 1 to 768, as said below
- handed: int32 [256], P(('seq', 'grp')), may hold values from 0 to 256, as said below
Outputs:
- window_share: float32 [131072, 256], P(('seq', 'grp'))
- share_gap: float32 [131072, 256], P(('seq', 'grp'))
Inputs may be any that keep to these rules, and one draw needn't show every extreme that they name: `window_ends`: for each shard, its first window_count slots hold distinct offsets in rising order; the remaining slots hold 0. `window_count`: some shard has 768 windows in every draw. `handed`: at most the shard's window_count minus 1; 0 on the last shard of each group along grp; the windows a shard keeps plus those it receives number at most 512, and exactly 512 on some shard that passes 512 // 2 in every draw.
All inputs are finite; a program needn't handle non-finite values.
Results may differ from a plain program's by a relative error of at most 0.0003.
Values sent between devices are 32-bit elements; how exact they have to be, the bound alone decides.
A program may use at most 64 MiB of HBM per device.

v0:
```python
import jax
import jax.numpy as jnp
from jax import lax
from jax.sharding import Mesh
from jax.sharding import PartitionSpec as P

CODES = 256
WINDOW = 4096
SEQ_GRP = ("seq_0", "seq_1", "grp_0", "grp_1")
GRP = ("grp_0", "grp_1")


def filled_with(shard, identity):
    return jnp.zeros_like(shard) + jnp.asarray(identity, shard.dtype)


def entering(shard, axes, combine, identity):
    before = start = filled_with(shard, identity)
    so_far = shard
    for axis in reversed(axes):
        size, position = (lax.axis_size(axis), lax.axis_index(axis))
        pieces = lax.all_gather(so_far, axis)
        inside, so_far = (start, start)
        for k in range(size):
            passed = k < position
            so_far = combine(so_far, pieces[k])
            inside = jnp.where(passed, so_far, inside)
        before = combine(inside, before)
    return before


def from_behind(block, axis, distance):
    devices = range(lax.axis_size(axis))
    route = [(i - distance, i) for i in devices if i - distance in devices]
    return lax.ppermute(block, axis, route)


def event_counts(marks, points, block_len, label_shift):
    portions = marks.reshape(marks.shape[0] // block_len, block_len)
    anchors = jnp.arange(portions.shape[0], dtype=jnp.int32) * block_len
    labels = jnp.arange(CODES, dtype=jnp.int32) + label_shift
    offsets = jnp.arange(block_len, dtype=jnp.int32)

    def advance(total, inputs):
        portion, anchor = inputs
        onehot = (portion[:, None] == labels[None, :]).astype(jnp.bfloat16)
        before = ((anchor + offsets)[None, :] <= points[:, None]).astype(jnp.bfloat16)
        return (total + jnp.dot(before, onehot, preferred_element_type=jnp.float32), None)

    initial = jnp.zeros((points.shape[0], CODES), jnp.float32)
    return lax.scan(advance, initial, (portions, anchors))[0]


def add_rows(earlier, later):
    return earlier + later


def local(event_codes, window_ends, window_count, handed):
    shard_len = event_codes.shape[0]
    slot_total = window_ends.shape[0]
    out_rows = 2 * slot_total // 3
    handoff_rows = out_rows // 2
    block_len = min(512, shard_len)
    shard_index = lax.axis_index(SEQ_GRP)
    totals = event_counts(event_codes, jnp.full((1,), shard_len - 1, jnp.int32), block_len, 0)[0]
    offset = entering(totals, SEQ_GRP, add_rows, jnp.zeros_like(totals))
    starts = window_ends - WINDOW
    own_tally = event_counts(event_codes, jnp.concatenate([window_ends, starts]), block_len, 0)
    end_tally = own_tally[:slot_total]
    start_tally = own_tally[slot_total:]
    inside = (starts >= 0)[:, None]
    tail_marks = from_behind(event_codes[shard_len - WINDOW :] + 1, SEQ_GRP, 1)
    tail_points = jnp.concatenate([window_ends, jnp.full((1,), WINDOW - 1, jnp.int32)])
    tail_tally = event_counts(tail_marks, tail_points, min(512, WINDOW), 1)
    after_start = tail_tally[slot_total:] - tail_tally[:slot_total]
    window_tally = jnp.where(inside, end_tally - start_tally, end_tally + after_start)
    running = offset[None, :] + end_tally
    end_position = shard_index * shard_len + window_ends
    length = jnp.minimum(WINDOW, end_position + 1).astype(jnp.float32)
    share_rows = CODES * window_tally / length[:, None]
    gap_rows = share_rows - CODES * running / (end_position + 1).astype(jnp.float32)[:, None]
    kept_count = window_count[0] - handed[0]
    sent_ids = jnp.arange(handoff_rows, dtype=jnp.int32)
    source = jnp.clip(kept_count + sent_ids, 0, slot_total - 1)
    sending = (sent_ids < handed[0])[:, None]
    outgoing = (
        jnp.where(sending, share_rows[source], 0.0),
        jnp.where(sending, gap_rows[source], 0.0),
        handed.astype(jnp.float32),
    )
    got_share, got_gap, got_count = from_behind((outgoing[0], outgoing[1], outgoing[2]), GRP, 1)
    arrived = got_count[0].astype(jnp.int32)
    row_ids = jnp.arange(out_rows, dtype=jnp.int32)
    from_prior = (row_ids < arrived)[:, None]
    prior_slot = jnp.clip(row_ids, 0, handoff_rows - 1)
    own_slot = jnp.clip(row_ids - arrived, 0, slot_total - 1)
    own_valid = ((row_ids >= arrived) & (row_ids - arrived < kept_count))[:, None]
    window_share = jnp.where(
        from_prior, got_share[prior_slot], jnp.where(own_valid, share_rows[own_slot], 0.0)
    )
    share_gap = jnp.where(
        from_prior, got_gap[prior_slot], jnp.where(own_valid, gap_rows[own_slot], 0.0)
    )
    return (window_share, share_gap)


def solution(mesh):
    split = Mesh(mesh.devices.reshape(4, 8, 4, 2), ("seq_0", "seq_1", "grp_0", "grp_1"))
    return jax.shard_map(
        local,
        mesh=split,
        in_specs=(P(SEQ_GRP), P(SEQ_GRP), P(SEQ_GRP), P(SEQ_GRP)),
        out_specs=(P(SEQ_GRP, None), P(SEQ_GRP, None)),
        check_vma=False,
    )
```

profile of v0, /device:TPU:1, one launch (start us, length us, event | category | flops | bytes accessed | tf_op | source)
XLA Modules:
  0.0 150.2 jit_solution(17924047392213165921)
XLA Ops:
  1.4 4.5 %collective-permute-start.1 = (s32[4096]{0:T(1024)S(1)}, s32[4096]{0:T(1024)S(1)}, u32[]{:S(2)}, u32[]{:S(2)}) collective-permute-start(s32[4096]{0:T(1024)S(1)} %slice_add_fusion), channel_id=1, source_target_pairs={{0,1},{1,2},{2,3},{3,4},{4,5},{5,6},{6,7},{7,8},{8,9},{9,10},{10,1... | collective-permute-start | bytes 49160 | tf_op jit(solution)/shard_map/ppermute | solution.py:35
  6.5 2.6 %collective-permute-start = (f32[1]{0:T(128)}, f32[1]{0:T(128)}, u32[]{:S(2)}, u32[]{:S(2)}) collective-permute-start(f32[1]{0:T(128)} %convert_element_type.21), channel_id=1, source_target_pairs={{0,1},{1,2},{2,3},{3,4},{4,5},{5,6},{6,7},{8,9},{9,10},{10,11},{11... | collective-permute-start | bytes 20 | tf_op jit(solution)/shard_map/ppermute | solution.py:35
  10.0 22.7 %while.35 = (s32[]{:T(128)}, f32[1,256]{1,0:T(1,128)S(1)}, s32[16]{0:T(128)S(1)}, s32[16,512]{1,0:T(8,128)S(1)}, s32[]{:T(128)}, /*index=5*/s32[]{:T(128)}) while((s32[]{:T(128)}, f32[1,256]{1,0:T(1,128)S(1)}, s32[16]{0:T(128)S(1)}, s32[16,512]{1,0:T(8,128)S(1)}, s32[]{:T(128)}, /*index=5*/s32[]{:T(128)}) %tuple.70), condition=%wide.region_5.6_spmd.clone, body=%wide.region_4.5_spmd.clone.sunk | while | flops 394755 | bytes 10339 | solution.py:51
  32.7 2.2 %all-gather = f32[2,1,256]{2,1,0:T(1,128)S(1)} all-gather(f32[1,1,256]{2,1,0:T(1,128)S(1)} %bitcast.94), channel_id=1, replica_groups=mesh['seq_0'=4,'seq_1'=8,'grp_0'=4,'grp_1'=2] {'grp_1'}, dimensions={0}, use_global_device_ids=true | all-gather | bytes 3072 | tf_op jit(solution)/shard_map/all_gather | solution.py:22
  34.9 8.0 %all-gather.1 = f32[4,1,256]{2,1,0:T(1,128)S(1)} all-gather(f32[1,1,256]{2,1,0:T(1,128)S(1)} %slice_add_fusion.10), channel_id=1, replica_groups=mesh['seq_0'=4,'seq_1'=8,'grp_0'=4,'grp_1'=2] {'grp_0'}, dimensions={0}, use_global_device_ids=true | all-gather | bytes 5120 | tf_op jit(solution)/shard_map/all_gather | solution.py:22
  42.9 13.8 %all-gather.2 = f32[8,1,256]{2,1,0:T(1,128)S(1)} all-gather(f32[1,1,256]{2,1,0:T(1,128)S(1)} %slice_add_fusion.7), channel_id=1, replica_groups=mesh['seq_0'=4,'seq_1'=8,'grp_0'=4,'grp_1'=2] {'seq_1'}, dimensions={0}, use_global_device_ids=true | all-gather | bytes 9216 | tf_op jit(solution)/shard_map/all_gather | solution.py:22
  56.7 8.0 %all-gather.3 = f32[4,1,256]{2,1,0:T(1,128)S(1)} all-gather(f32[1,1,256]{2,1,0:T(1,128)S(1)} %bitcast.89), channel_id=1, replica_groups=mesh['seq_0'=4,'seq_1'=8,'grp_0'=4,'grp_1'=2] {'seq_0'}, dimensions={0}, use_global_device_ids=true | all-gather | bytes 5120 | tf_op jit(solution)/shard_map/all_gather | solution.py:22
  66.8 41.1 %while.33 = (s32[]{:T(128)}, f32[1536,256]{1,0:T(8,128)S(1)}, s32[16]{0:T(128)S(1)}, s32[1536]{0:T(1024)S(1)}, s32[16,512]{1,0:T(8,128)S(1)}, /*index=5*/s32[]{:T(128)}, s32[]{:T(128)}) while((s32[]{:T(128)}, f32[1536,256]{1,0:T(8,128)S(1)}, s32[16]{0:T(128)S(1)}, s32[1536]{0:T(1024)S(1)}, s32[16,512]{1,0:T(8,128)S(1)}, ...), condition=%wide.region_1.2_spmd.clone, body=%wide.region_0.1_spmd.clone.sunk | while | flops 404357632 | bytes 3162219 | solution.py:51
  68.1 1.3 fusion.54
  70.6 1.3 fusion.54
  78.3 1.3 fusion.54
  83.5 1.3 fusion.54
  88.6 1.3 fusion.54
  93.8 1.3 fusion.54
  98.9 1.3 fusion.54
  104.0 1.3 fusion.54
  109.3 16.0 %while.34 = (s32[]{:T(128)}, f32[769,256]{1,0:T(8,128)S(1)}, s32[8]{0:T(128)S(1)}, s32[769]{0:T(1024)S(1)}, s32[8,512]{1,0:T(8,128)S(1)}, /*index=5*/s32[]{:T(128)}, s32[]{:T(128)}) while((s32[]{:T(128)}, f32[769,256]{1,0:T(8,128)S(1)}, s32[8]{0:T(128)S(1)}, s32[769]{0:T(1024)S(1)}, s32[8,512]{1,0:T(8,128)S(1)}, ...), condition=%wide.region_3.4_spmd.clone, body=%wide.region_2.3_spmd.clone.sunk | while | flops 202508032 | bytes 1590383 | solution.py:51
  126.2 1.5 %divide_subtract_fusion = (f32[768,256]{1,0:T(8,128)S(1)}, f32[768,256]{1,0:T(8,128)S(1)}) fusion(f32[1536,256]{1,0:T(8,128)S(1)} %get-tuple-element.108, f32[768]{0:T(1024)S(1)} %get-tuple-element.207, f32[256]{0:T(256)S(1)} %bitcast.92, f32[768]{0:T(1024)S(1)} %get-tuple-element.206, f32[769,256]{1,0:T(8,128)} %copy-done, f32[256]{0:T(256)S(1)} %bitcast.93, ...), kind=kLoop, calls=%fused_computation.39 | loop fusion | flops 1966080 | bytes 3941120 | tf_op jit(solution)/shard_map/sub | solution.py:81
  130.5 10.2 %collective-permute-start.2 = (f32[256,256]{1,0:T(8,128)}, f32[256,256]{1,0:T(8,128)S(1)}, u32[]{:S(2)}, u32[]{:S(2)}) collective-permute-start(f32[256,256]{1,0:T(8,128)} %get-tuple-element.212), channel_id=1, source_target_pairs={{0,1},{1,2},{2,3},{3,4},{4,5},{5,6},{6,7},{8,9},{9,10},{10,11},{11... | collective-permute-start | bytes 786440 | tf_op jit(solution)/shard_map/ppermute | solution.py:35
  140.7 1.9 %collective-permute-start.3 = (f32[256,256]{1,0:T(8,128)S(1)}, f32[256,256]{1,0:T(8,128)S(1)}, u32[]{:S(2)}, u32[]{:S(2)}) collective-permute-start(f32[256,256]{1,0:T(8,128)S(1)} %get-tuple-element.211), channel_id=1, source_target_pairs={{0,1},{1,2},{2,3},{3,4},{4,5},{5,6},{6,7},{8,9},{9,10},{10,11},{11... | collective-permute-start | bytes 786440 | tf_op jit(solution)/shard_map/ppermute | solution.py:35
  142.7 1.6 %gather_fusion.2 = f32[512,256]{1,0:T(8,128)S(1)} fusion(f32[768,256]{1,0:T(8,128)S(1)} %get-tuple-element.203, s32[1024]{0:T(1024)S(1)} %pad_clamp_fusion), kind=kCustom, calls=%fused_computation.2 | custom fusion | bytes 1050624 | tf_op jit(solution)/shard_map/gather | solution.py:99
  144.3 1.6 %gather_fusion.5 = f32[512,256]{1,0:T(8,128)S(1)} fusion(f32[768,256]{1,0:T(8,128)S(1)} %get-tuple-element.202, s32[1024]{0:T(1024)S(1)} %pad_clamp_fusion), kind=kCustom, calls=%fused_computation.5 | custom fusion | bytes 1050624 | tf_op jit(solution)/shard_map/gather | solution.py:102
  145.9 1.6 %gather_fusion.1 = f32[512,256]{1,0:T(8,128)S(1)} fusion(f32[256,256]{1,0:T(8,128)S(1)} %collective-permute-done.2, s32[1024]{0:T(1024)S(1)} %pad_clamp_fusion.1), kind=kCustom, calls=%fused_computation.1 | custom fusion | bytes 1050624 | tf_op jit(solution)/shard_map/gather | solution.py:99
  147.5 1.6 %gather_fusion.4 = f32[512,256]{1,0:T(8,128)S(1)} fusion(f32[256,256]{1,0:T(8,128)S(1)} %collective-permute-done.3, s32[1024]{0:T(1024)S(1)} %pad_clamp_fusion.1), kind=kCustom, calls=%fused_computation.4 | custom fusion | bytes 1050624 | tf_op jit(solution)/shard_map/gather | solution.py:102
  (213 shorter events, 76.6 us)
Async XLA Ops:
  1.4 108.0 %collective-permute-start.1 = (s32[4096]{0:T(1024)S(1)}, s32[4096]{0:T(1024)S(1)}, u32[]{:S(2)}, u32[]{:S(2)}) collective-permute-start(s32[4096]{0:T(1024)S(1)} %slice_add_fusion), channel_id=1, source_target_pairs={{0,1},{1,2},{2,3},{3,4},{4,5},{5,6},{6,7},{7,8},{8,9},{9,10},{10,1... | collective-permute-start | bytes 49160 | tf_op jit(solution)/shard_map/ppermute | solution.py:35
  6.5 102.2 %collective-permute-start = (f32[1]{0:T(128)}, f32[1]{0:T(128)}, u32[]{:S(2)}, u32[]{:S(2)}) collective-permute-start(f32[1]{0:T(128)} %convert_element_type.21), channel_id=1, source_target_pairs={{0,1},{1,2},{2,3},{3,4},{4,5},{5,6},{6,7},{8,9},{9,10},{10,11},{11... | collective-permute-start | bytes 20 | tf_op jit(solution)/shard_map/ppermute | solution.py:35
  66.8 41.1 %copy-start.1 = (s32[768]{0:T(1024)S(1)}, s32[768]{0:T(1024)}, u32[]{:S(2)}) copy-start(s32[768]{0:T(1024)} %param.11) | copy-start | bytes 9220
  125.3 0.9 copy-start
  130.5 15.4 %collective-permute-start.2 = (f32[256,256]{1,0:T(8,128)}, f32[256,256]{1,0:T(8,128)S(1)}, u32[]{:S(2)}, u32[]{:S(2)}) collective-permute-start(f32[256,256]{1,0:T(8,128)} %get-tuple-element.212), channel_id=1, source_target_pairs={{0,1},{1,2},{2,3},{3,4},{4,5},{5,6},{6,7},{8,9},{9,10},{10,11},{11... | collective-permute-start | bytes 786440 | tf_op jit(solution)/shard_map/ppermute | solution.py:35
  140.7 6.7 %collective-permute-start.3 = (f32[256,256]{1,0:T(8,128)S(1)}, f32[256,256]{1,0:T(8,128)S(1)}, u32[]{:S(2)}, u32[]{:S(2)}) collective-permute-start(f32[256,256]{1,0:T(8,128)S(1)} %get-tuple-element.211), channel_id=1, source_target_pairs={{0,1},{1,2},{2,3},{3,4},{4,5},{5,6},{6,7},{8,9},{9,10},{10,11},{11... | collective-permute-start | bytes 786440 | tf_op jit(solution)/shard_map/ppermute | solution.py:35
where the time goes:
time: 151 us; the launch traced here: 150 us
  local copies, waits for them, and re-layouts  33.8 us (22%)
  blocking collectives  32 us (21%)
  other arithmetic  30.6 us (20%)
  matrix products  30.2 us (20%)
  starting transfers between devices  19.3 us (13%)
  between operations  2.87 us (2%)
    all_gather x4, blocking collectives, entering(): pieces = lax.all_gather(so_far, axis)  32 us
    dot_general x40, matrix products, advance(): jnp.dot(before, onehot, preferred_element_type=jnp.float32)  30.2 us
    dynamic_slice x80, local copies, waits for them, and re-layouts, event_counts(): return lax.scan(advance, initial, (portions, anchors))[0]  23.8 us
    ppermute x4, starting transfers between devices, from_behind(): return lax.ppermute(block, axis, route)  19.3 us
    add x24, other arithmetic, advance(): anchor + offsets  15.4 us
    le x16, other arithmetic, advance(): (anchor + offsets)[None, :] <= points[:, None]  8.79 us
  transfers between devices with their start and end apart: 4, of which 0 were waited for; matrix products, arithmetic and copies ran while one was open for 47% of the time, Pallas kernels for 0%

commit v1 on v0

v1 whole, which is shorter than its diff:
```python
import functools

import jax
import jax.numpy as jnp
from jax import lax
from jax.experimental import pallas as pl
from jax.experimental.pallas import tpu as pltpu
from jax.sharding import PartitionSpec as P

CODES = 256
WINDOW = 4096
SHARD = 8192
CAP = 512
SLOTS = 768
HAND = CAP // 2
NY, NZ, NG = 4, 8, 8
PLANE = NY * NG
NSHARDS = NY * NZ * NG
LANES = 128
ROWS = SHARD // LANES
STEP = 1024
MESH = pl.DeviceIdType.MESH
NT = (((1,), (1,)), ((), ()))
F32 = jnp.float32
BF16 = jnp.bfloat16


def device_of(shard):
    return (shard // NG, shard % NG)


def one_hot(row):
    wide = jnp.broadcast_to(row.astype(F32), (16, LANES)).astype(BF16)
    wide = jnp.concatenate([wide] * (CODES // 16), axis=0)
    label = lax.broadcasted_iota(jnp.int32, (CODES, LANES), 0).astype(F32).astype(BF16)
    return jnp.where(wide == label, jnp.ones((), BF16), jnp.zeros((), BF16))


def one_hot_block(block):
    return jnp.concatenate([one_hot(block[i : i + 1]) for i in range(8)], axis=1)


def marks(ends, base, later):
    n = ends.shape[0]
    pieces = []
    for i in range(STEP // LANES):
        at = lax.broadcasted_iota(jnp.int32, (16, LANES), 1) + (base + i * LANES)
        at = jnp.concatenate([at.astype(jnp.int16)] * (n // 16), axis=0)
        hit = at > ends if later else at <= ends
        pieces.append(jnp.where(hit, jnp.ones((), BF16), jnp.zeros((), BF16)))
    return jnp.concatenate(pieces, axis=1)


def end_rows(note, first, n):
    line = jnp.concatenate([note[i : i + 1] for i in range(SLOTS // LANES)], axis=1)
    high = (line >> 8).astype(F32)
    low = (line & 255).astype(F32)
    both = jnp.concatenate(
        [jnp.broadcast_to(high, (LANES, SLOTS)), jnp.broadcast_to(low, (LANES, SLOTS))], axis=0
    ).astype(BF16)
    slot = lax.broadcasted_iota(jnp.int32, (n, SLOTS), 1)
    row = lax.broadcasted_iota(jnp.int32, (n, SLOTS), 0)
    pick = jnp.where(slot == row + first, 1.0, 0.0).astype(BF16)
    got = lax.dot_general(pick, both, NT, preferred_element_type=F32)
    return (got[:, :LANES] * 256.0 + got[:, LANES:]).astype(jnp.int32)


def dot_nt(a, b):
    return lax.dot_general(a, b, NT, preferred_element_type=F32)


def tally_kernel(
    codes_hbm, ends_hbm, count_ref, handed_ref,
    share_ref, run_ref, inv_ref, off_ref, arr_ref,
    own, prev, prior, note, got, mine, plane, sums, column, own_acc, tail_acc, got_acc,
    load_sem, p1_send, p1_recv, p2_send, p2_recv, pass_send, pass_recv,
):
    seq, grp = lax.axis_index("seq"), lax.axis_index("grp")
    y, z = seq // NZ, seq % NZ
    shard = seq * NG + grp
    spot = y * NG + grp

    load_codes = pltpu.make_async_copy(codes_hbm, own, load_sem.at[0])
    load_ends = pltpu.make_async_copy(ends_hbm, note.at[pl.ds(0, 6)], load_sem.at[1])
    load_codes.start()
    load_ends.start()

    barrier = pltpu.get_barrier_semaphore()

    def plane_peer(k):
        at = (spot + k) % PLANE
        return ((at // NG) * NZ + z, at % NG)

    def column_peer(k):
        return (y * NZ + (z + k) % NZ, grp)

    for k in range(1, PLANE):
        pl.semaphore_signal(barrier, inc=1, device_id=plane_peer(k), device_id_type=MESH)
    for k in range(1, NZ):
        pl.semaphore_signal(barrier, inc=1, device_id=column_peer(k), device_id_type=MESH)
    for back in (1, 2):
        @pl.when(shard >= back)
        def _():
            pl.semaphore_signal(barrier, inc=1, device_id=device_of(shard - back), device_id_type=MESH)

    note[6:7] = jnp.full((1, LANES), count_ref[0], jnp.int32)
    note[7:8] = jnp.full((1, LANES), handed_ref[0], jnp.int32)
    own_acc[...] = jnp.zeros_like(own_acc)
    tail_acc[...] = jnp.zeros_like(tail_acc)
    got_acc[...] = jnp.zeros_like(got_acc)

    load_codes.wait()

    def count_rows(i, total):
        block = own[pl.ds(pl.multiple_of(i * 8, 8), 8)]
        for j in range(8):
            total = total + one_hot(block[j : j + 1])
        return total

    spread = lax.fori_loop(0, ROWS // 8, count_rows, jnp.zeros((CODES, LANES), BF16))
    total = dot_nt(jnp.ones((8, LANES), BF16), spread)[0:1]
    mine[0] = total
    plane[spot] = total

    load_ends.wait()
    own_ends = end_rows(note[...], 0, CAP)
    ends16 = own_ends.astype(jnp.int16)
    starts16 = (own_ends - WINDOW).astype(jnp.int16)

    def first_half(i):
        codes = one_hot_block(own[pl.ds(pl.multiple_of(i * 8, 8), 8)])
        rows = jnp.concatenate([marks(ends16, i * STEP, False), marks(starts16, i * STEP, False)], axis=0)
        own_acc[...] += dot_nt(rows, codes)

    def second_half(i):
        codes = one_hot_block(own[pl.ds(pl.multiple_of(i * 8, 8), 8)])
        own_acc[pl.ds(0, CAP)] += dot_nt(marks(ends16, i * STEP, False), codes)

    pl.loop(0, 2)(first_half)

    pl.semaphore_wait(barrier, PLANE - 1 + NZ - 1 + jnp.minimum(NSHARDS - 1 - shard, 2))

    sends = []
    for k in range(1, PLANE):
        sends.append(pltpu.make_async_remote_copy(
            src_ref=mine.at[0], dst_ref=plane.at[spot], send_sem=p1_send.at[k], recv_sem=p1_recv.at[k],
            device_id=plane_peer(k), device_id_type=MESH))
    for send in sends:
        send.start()

    pass_codes = pltpu.make_async_remote_copy(
        src_ref=own, dst_ref=prev, send_sem=pass_send.at[0], recv_sem=pass_recv.at[0],
        device_id=device_of(jnp.minimum(shard + 1, NSHARDS - 1)), device_id_type=MESH)
    pass_note = pltpu.make_async_remote_copy(
        src_ref=note, dst_ref=got, send_sem=pass_send.at[1], recv_sem=pass_recv.at[1],
        device_id=device_of(jnp.minimum(shard + 1, NSHARDS - 1)), device_id_type=MESH)
    pass_tail = pltpu.make_async_remote_copy(
        src_ref=own.at[pl.ds(ROWS // 2, ROWS // 2)], dst_ref=prior, send_sem=pass_send.at[2], recv_sem=pass_recv.at[2],
        device_id=device_of(jnp.minimum(shard + 2, NSHARDS - 1)), device_id_type=MESH)

    @pl.when(shard + 1 < NSHARDS)
    def _():
        pass_note.start()
        pass_codes.start()

    @pl.when(shard + 2 < NSHARDS)
    def _():
        pass_tail.start()

    pl.loop(2, 4)(first_half)
    pl.loop(4, 8)(second_half)

    for send in sends:
        send.wait_recv()

    below = jnp.zeros((1, CODES), F32)
    level = jnp.zeros((1, CODES), F32)
    inside = jnp.zeros((1, CODES), F32)
    before = jnp.zeros((1, CODES), F32)
    for k in range(PLANE):
        part = plane[k]
        below = below + jnp.where(k // NG < y, part, 0.0)
        here = jnp.where(k // NG == y, part, 0.0)
        level = level + here
        inside = inside + jnp.where(k % NG < grp, here, 0.0)
        before = before + jnp.where(k % NG == grp - 1, here, 0.0)
    sums[0] = below
    sums[1] = below + level

    climbs = []
    for k in range(1, NZ):
        after = ((z + k) % NZ > z).astype(jnp.int32)
        climbs.append(pltpu.make_async_remote_copy(
            src_ref=sums.at[after], dst_ref=column.at[z], send_sem=p2_send.at[k], recv_sem=p2_recv.at[k],
            device_id=column_peer(k), device_id_type=MESH))
    for climb in climbs:
        climb.start()
    column[z] = below + inside

    @pl.when(shard >= 1)
    def _():
        pass_note.wait_recv()
        pass_codes.wait_recv()

    @pl.when(shard >= 2)
    def _():
        pass_tail.wait_recv()

    arrived = jnp.where(grp > 0, got[7:8], 0)
    arr_ref[...] = jnp.broadcast_to(arrived, (8, LANES))
    first = jnp.concatenate([got[6:7] - arrived] * (SLOTS // LANES), axis=1)
    got_ends = end_rows(got[...], first, HAND)
    gends16 = got_ends.astype(jnp.int16)
    gstarts16 = (got_ends - WINDOW).astype(jnp.int16)

    def prev_first(i):
        block = jnp.where(shard >= 1, prev[pl.ds(pl.multiple_of(i * 8, 8), 8)], -1)
        rows = jnp.concatenate([marks(gends16, i * STEP, False), marks(gstarts16, i * STEP, False)], axis=0)
        got_acc[pl.ds(0, 2 * HAND)] += dot_nt(rows, one_hot_block(block))

    def prev_second(i):
        block = jnp.where(shard >= 1, prev[pl.ds(pl.multiple_of(i * 8, 8), 8)], -1)
        rows = jnp.concatenate(
            [marks(gends16, i * STEP, False), marks(ends16, i * STEP - WINDOW, True)], axis=0)
        part = dot_nt(rows, one_hot_block(block))
        got_acc[pl.ds(0, HAND)] += part[:HAND]
        tail_acc[...] += part[HAND:]

    def prior_part(i):
        block = jnp.where(shard >= 2, prior[pl.ds(pl.multiple_of(i * 8, 8), 8)], -1)
        got_acc[pl.ds(2 * HAND, HAND)] += dot_nt(marks(gends16, i * STEP, True), one_hot_block(block))

    pl.loop(0, 4)(prev_first)
    pl.loop(4, 8)(prev_second)
    pl.loop(0, 4)(prior_part)

    def finish(at, n, ends, origin, held, window, earlier):
        upto = (ends + (origin * SHARD + 1)).astype(F32)
        inv = 256.0 / upto
        scale = 256.0 / jnp.minimum(upto, float(WINDOW))
        inv_ref[pl.ds(at, n)] = inv
        share_ref[pl.ds(at, n)] = window * jnp.concatenate([scale, scale], axis=1)
        run_ref[pl.ds(at, n)] = (held - earlier) * jnp.concatenate([inv, inv], axis=1)

    held = got_acc[pl.ds(0, HAND)]
    finish(0, HAND, got_ends, shard - 1, held,
           held - got_acc[pl.ds(HAND, HAND)] + got_acc[pl.ds(2 * HAND, HAND)], before)
    held = own_acc[pl.ds(0, CAP)]
    finish(HAND, CAP, own_ends, shard, held,
           held - own_acc[pl.ds(CAP, CAP)] + tail_acc[...], jnp.zeros((1, CODES), F32))

    for climb in climbs:
        climb.wait_recv()
    offset = column[0]
    for k in range(1, NZ):
        offset = offset + column[k]
    off_ref[...] = jnp.broadcast_to(offset, (8, CODES))

    for send in sends:
        send.wait_send()
    for climb in climbs:
        climb.wait_send()

    @pl.when(shard + 1 < NSHARDS)
    def _():
        pass_note.wait_send()
        pass_codes.wait_send()

    @pl.when(shard + 2 < NSHARDS)
    def _():
        pass_tail.wait_send()


def place_kernel(
    count_ref, handed_ref, share_ref, run_ref, inv_ref, off_ref, arr_ref,
    share_hbm, gap_hbm, share_buf, gap_buf, sem,
):
    arrived = jnp.max(arr_ref[0:1, 0:1])
    kept = count_ref[0] - handed_ref[0]
    offset = off_ref[0:1]
    n = LANES
    copies = []
    for i in range(CAP // n):
        row = lax.broadcasted_iota(jnp.int32, (n, CODES), 0) + i * n
        start = HAND + i * n - arrived
        whole = jnp.minimum(start // 8 * 8, HAND + CAP - n - 8)
        rest = start - whole

        def rows_at(begin, n):
            inv = inv_ref[pl.ds(begin, n)]
            share = share_ref[pl.ds(begin, n)]
            run = run_ref[pl.ds(begin, n)] + jnp.concatenate([inv, inv], axis=1) * offset
            return share, share - run

        share, gap = rows_at(pl.multiple_of(whole, 8), n + 8)
        share = pltpu.roll(share, n + 8 - rest, 0)[:n]
        gap = pltpu.roll(gap, n + 8 - rest, 0)[:n]
        valid = row - arrived < kept
        share = jnp.where(valid, share, 0.0)
        gap = jnp.where(valid, gap, 0.0)
        if i * n < HAND:
            early_share, early_gap = rows_at(i * n, n)
            share = jnp.where(row < arrived, early_share, share)
            gap = jnp.where(row < arrived, early_gap, gap)
        share_buf[pl.ds(i * n, n)] = share
        gap_buf[pl.ds(i * n, n)] = gap
        for j, (buf, out) in enumerate(((share_buf, share_hbm), (gap_buf, gap_hbm))):
            copy = pltpu.make_async_copy(buf.at[pl.ds(i * n, n)], out.at[pl.ds(i * n, n)], sem.at[j, i])
            copy.start()
            copies.append(copy)
    for copy in copies:
        copy.wait()


def local(event_codes, window_ends, window_count, handed):
    vmem = pl.BlockSpec(memory_space=pltpu.VMEM)
    smem = pl.BlockSpec(memory_space=pltpu.SMEM)
    hbm = pl.BlockSpec(memory_space=pl.ANY)
    far = pl.BlockSpec(memory_space=pltpu.HBM)
    total = HAND + CAP
    dma = pltpu.SemaphoreType.DMA
    tallies = pl.pallas_call(
        tally_kernel,
        out_shape=(
            jax.ShapeDtypeStruct((total, CODES), F32),
            jax.ShapeDtypeStruct((total, CODES), F32),
            jax.ShapeDtypeStruct((total, LANES), F32),
            jax.ShapeDtypeStruct((8, CODES), F32),
            jax.ShapeDtypeStruct((8, LANES), jnp.int32),
        ),
        in_specs=[far, far, smem, smem],
        out_specs=(vmem,) * 5,
        scratch_shapes=[
            pltpu.VMEM((ROWS, LANES), jnp.int32),
            pltpu.VMEM((ROWS, LANES), jnp.int32),
            pltpu.VMEM((ROWS // 2, LANES), jnp.int32),
            pltpu.VMEM((8, LANES), jnp.int32),
            pltpu.VMEM((8, LANES), jnp.int32),
            pltpu.VMEM((1, 1, CODES), F32),
            pltpu.VMEM((PLANE, 1, CODES), F32),
            pltpu.VMEM((2, 1, CODES), F32),
            pltpu.VMEM((NZ, 1, CODES), F32),
            pltpu.VMEM((2 * CAP, CODES), F32),
            pltpu.VMEM((CAP, CODES), F32),
            pltpu.VMEM((3 * HAND, CODES), F32),
            dma((2,)), dma((PLANE,)), dma((PLANE,)), dma((NZ,)), dma((NZ,)), dma((3,)), dma((3,)),
        ],
        compiler_params=pltpu.CompilerParams(
            collective_id=0, has_side_effects=True, vmem_limit_bytes=32 * 2**20),
        name="tally",
    )(event_codes.reshape(ROWS, LANES), window_ends.reshape(SLOTS // LANES, LANES), window_count, handed)
    return pl.pallas_call(
        place_kernel,
        out_shape=(jax.ShapeDtypeStruct((CAP, CODES), F32),) * 2,
        in_specs=[smem, smem] + [vmem] * 5,
        out_specs=(hbm, hbm),
        scratch_shapes=[pltpu.VMEM((CAP, CODES), F32), pltpu.VMEM((CAP, CODES), F32), dma((2, CAP // LANES))],
        compiler_params=pltpu.CompilerParams(vmem_limit_bytes=16 * 2**20),
        name="place",
    )(window_count, handed, *tallies)


def solution(mesh):
    both = ("seq", "grp")
    return jax.shard_map(
        local,
        mesh=mesh,
        in_specs=(P(both), P(both), P(both), P(both)),
        out_specs=(P(both, None), P(both, None)),
        check_vma=False,
    )
```

time: 151 us -> 27.7 us (0.18)
  local copies, waits for them, and re-layouts: 33.8 us -> 0.76 us
  blocking collectives: 32 us -> 0 us
  other arithmetic: 30.6 us -> 0 us
  matrix products: 30.2 us -> 0 us
  Pallas kernels: 0 us -> 24.8 us
  starting transfers between devices: 19.3 us -> 0 us
    all_gather x4 -> x0, blocking collectives: 32 us -> none  [entering(): pieces = lax.all_gather(so_far, axis)]
    dot_general x40 -> x0, matrix products: 30.2 us -> none  [advance(): jnp.dot(before, onehot, preferred_element_type=jnp.float32)]
    pallas_call x0 -> x2, Pallas kernels: none -> 24.8 us  [the longest x1 23.5 us: local(): pl.pallas_call(tally_kernel, out_shape=(jax.ShapeDtypeStruct((total, CODE...]
    dynamic_slice x80 -> x0, local copies, waits for them, and re-layouts: 23.8 us -> none  [event_counts(): return lax.scan(advance, initial, (portions, anchors))[0]]
    ppermute x4 -> x0, starting transfers between devices: 19.3 us -> none  [from_behind(): return lax.ppermute(block, axis, route)]
    add x37 -> x0, other arithmetic: 16.2 us -> none  [the longest x24 15.4 us: advance(): anchor + offsets]
    le x16 -> x0, other arithmetic: 8.79 us -> none  [advance(): (anchor + offsets)[None, :] <= points[:, None]]
    gather x6 -> x0, local copies, waits for them, and re-layouts: 8.23 us -> none  [the longest x1 1.57 us: local(): gap_rows[own_slot]]
  transfers between devices with their start and end apart: 4 -> 0, of which waited for: 0 -> 0; matrix products, arithmetic and copies ran while one was open for 47% -> 0% of each run, Pallas kernels for 0% -> 0%
where the time goes in v1:
time: 27.7 us; the launch traced here: 27.5 us
  Pallas kernels  24.8 us (90%)
  between operations  1.97 us (7%)
  local copies, waits for them, and re-layouts  0.76 us (3%)
    pallas_call x1, Pallas kernels, local(): pl.pallas_call(tally_kernel, out_shape=(jax.ShapeDtypeStruct((total, CODE...  23.5 us
    pallas_call x1, Pallas kernels, local(): pl.pallas_call(place_kernel, out_shape=(jax.ShapeDtypeStruct((CAP, CODES)...  1.33 us
    unnamed x4, local copies, waits for them, and re-layouts  0.76 us

profile of v1, /device:TPU:1, one launch (start us, length us, event | category | flops | bytes accessed | tf_op | source)
XLA Modules:
  0.0 27.5 jit_solution(13375668189542872098)
XLA Ops:
  0.6 0.0 copy-start.1
  1.9 0.0 copy-done.1
  2.0 0.0 copy-start
  2.0 0.7 %copy-done = s32[8192]{0:T(1024)S(1)} copy-done((s32[8192]{0:T(1024)S(1)}, s32[8192]{0:T(1024)}, u32[]{:S(2)}) %copy-start) | copy-done | bytes 32792
  2.7 23.5 %tally.1 = (f32[768,256]{1,0:T(8,128)S(1)}, f32[768,256]{1,0:T(8,128)S(1)}, f32[768,128]{1,0:T(8,128)S(1)}, f32[8,256]{1,0:T(8,128)S(1)}, s32[8,128]{1,0:T(8,128)S(1)}) custom-call(s32[64,128]{1,0:T(8,128)S(1)} %bitcast.2, s32[6,128]{1,0:T(8,128)S(1)} %bitcast.3, s32[1]{0:T(128)S(6)} %copy.6.count_ref, s32[1]{0:T(128)S(6)} %copy.7.handed_ref), custom_call_target="tpu_custom_call" | custom-call | tf_op jit(solution)/shard_map/tally/pallas_call | solution.py:322
  26.2 1.3 %place.1 = (f32[512,256]{1,0:T(8,128)}, f32[512,256]{1,0:T(8,128)}) custom-call(s32[1]{0:T(128)S(6)} %copy.6.count_ref, s32[1]{0:T(128)S(6)} %copy.7.handed_ref, f32[768,256]{1,0:T(8,128)S(1)} %get-tuple-element.7.share_ref, f32[768,256]{1,0:T(8,128)S(1)} %get-tuple-element.8.run_ref, f32[768,128]{1,0:T(8,128)S(1)} %get-tuple-element.9.inv_ref, ...), custom_call_target="tpu_custom_call" | custom-call | tf_op jit(solution)/shard_map/place/pallas_call | solution.py:352
Async XLA Ops:
  0.6 1.3 %copy-start.1 = (s32[768]{0:T(1024)S(1)}, s32[768]{0:T(1024)}, u32[]{:S(2)}) copy-start(s32[768]{0:T(1024)} %param.5) | copy-start | bytes 9220
  2.0 0.8 %copy-start = (s32[8192]{0:T(1024)S(1)}, s32[8192]{0:T(1024)}, u32[]{:S(2)}) copy-start(s32[8192]{0:T(1024)} %param.4) | copy-start | bytes 98308

commit v2 on v1

v2 whole, which is shorter than its diff:
```python
import functools

import jax
import jax.numpy as jnp
from jax import lax
from jax.experimental import pallas as pl
from jax.experimental.pallas import tpu as pltpu
from jax.sharding import PartitionSpec as P

CODES = 256
WINDOW = 4096
SHARD = 8192
CAP = 512
SLOTS = 768
HAND = CAP // 2
NY, NZ, NG = 4, 8, 8
PLANE = NY * NG
NSHARDS = NY * NZ * NG
LANES = 128
ROWS = SHARD // LANES
BLOCK = 16
HALF_BLOCKS = SHARD // BLOCK // 2
MESH = pl.DeviceIdType.MESH
NT = (((1,), (1,)), ((), ()))
F32 = jnp.float32
BF16 = jnp.bfloat16


def device_of(shard):
    return (shard // NG, shard % NG)


def one_hot(row):
    wide = jnp.broadcast_to(row, (16, LANES)).astype(BF16)
    wide = jnp.concatenate([wide] * (CODES // 16), axis=0)
    label = lax.broadcasted_iota(jnp.int32, (CODES, LANES), 0).astype(F32).astype(BF16)
    return jnp.where(wide == label, jnp.ones((), BF16), jnp.zeros((), BF16))


def by_block(half):
    half = half.astype(F32)
    turned = [half] + [pltpu.roll(half, LANES - 32 * k, 1) for k in (1, 2, 3)]
    return jnp.transpose(jnp.concatenate(turned, axis=0))[:32]


def block_counts(rows):
    total = one_hot(rows[0:1])
    for i in range(1, BLOCK):
        total = total + one_hot(rows[i : i + 1])
    return total


def block_column():
    at = lax.broadcasted_iota(jnp.int32, (HALF_BLOCKS, HAND), 0)
    return (8 * (at & 31) + ((at >> 5) & 3) * 2 + (at >> 7)).astype(jnp.int16)


def tall(row, n):
    wide = jnp.broadcast_to(row, (16, row.shape[1])).astype(jnp.int16)
    return jnp.concatenate([wide] * (n // 16), axis=0)


def flag(hit):
    return jnp.where(hit, jnp.ones((), BF16), jnp.zeros((), BF16))


def ends_line(note, slots, base):
    line = jnp.concatenate([note[i : i + 1] for i in range(slots // LANES)], axis=1)
    high = jnp.broadcast_to((line >> 8) + base, (8, slots))
    low = jnp.broadcast_to(line & 255, (8, slots))
    row = lax.broadcasted_iota(jnp.int32, (8, slots), 0)
    return jnp.where(row == 0, high, low).astype(F32).astype(BF16)


def picks(slots, first, at):
    slot = lax.broadcasted_iota(jnp.int32, (slots, HAND), 0)
    lane = lax.broadcasted_iota(jnp.int32, (slots, HAND), 1)
    return flag((slot - lane - at).astype(jnp.int16) == tall(first, slots))


def dot(a, b):
    return jnp.dot(a, b, preferred_element_type=F32)


def dot_nt(a, b):
    return lax.dot_general(a, b, NT, preferred_element_type=F32)


def tally_kernel(
    codes_hbm, ends_hbm, count_hbm, handed_hbm,
    share_ref, gap_ref, inv_ref, off_ref,
    own, prev, prior, note, got, mine, plane, sums, column, counts, blocks, scalars,
    load_sem, p1_send, p1_recv, p2_send, p2_recv, pass_send, pass_recv,
):
    seq, grp = lax.axis_index("seq"), lax.axis_index("grp")
    y, z = seq // NZ, seq % NZ
    shard = seq * NG + grp
    spot = y * NG + grp

    load_codes = pltpu.make_async_copy(codes_hbm, own, load_sem.at[0])
    load_ends = pltpu.make_async_copy(ends_hbm, note.at[pl.ds(0, 6)], load_sem.at[1])
    load_count = pltpu.make_async_copy(count_hbm, scalars.at[0], load_sem.at[2])
    load_handed = pltpu.make_async_copy(handed_hbm, scalars.at[1], load_sem.at[3])
    load_codes.start()
    load_ends.start()
    load_count.start()
    load_handed.start()

    barrier = pltpu.get_barrier_semaphore()

    def plane_device(dy, dg):
        return ((y + dy) * NZ + z, (grp + dg + NG) % NG)

    def column_device(k):
        return (y * NZ + (z + k + NZ) % NZ, grp)

    def climbs_to(k):
        return jnp.logical_or(y > 0, (z + k) % NZ > z)

    def climbs_from(k):
        return jnp.logical_or(y > 0, (z - k + NZ) % NZ < z)

    def greet(device):
        pl.semaphore_signal(barrier, inc=1, device_id=device, device_id_type=MESH)

    for dy in range(NY):
        @pl.when(y >= dy)
        def _():
            for dg in range(NG):
                if dy or dg:
                    greet(plane_device(-dy, -dg))
    for k in range(1, NZ):
        pl.when(climbs_from(k))(functools.partial(greet, column_device(-k)))
    for back in (1, 2):
        pl.when(shard >= back)(functools.partial(greet, device_of(shard - back)))

    def enter(half, codes):
        by = by_block(codes)
        first, second = block_counts(by[:BLOCK]), block_counts(by[BLOCK:])
        at = half * HALF_BLOCKS
        counts[:, at : at + LANES] = first
        counts[:, at + LANES : at + HALF_BLOCKS] = second
        blocks[:, at : at + LANES] = by[:BLOCK].astype(BF16)
        blocks[:, at + LANES : at + HALF_BLOCKS] = by[BLOCK:].astype(BF16)
        return first + second

    load_codes.wait()
    spread = enter(3, own[0:32]) + enter(4, own[32:64])
    total = dot_nt(jnp.ones((8, LANES), BF16), spread)[0:1]
    mine[0] = total
    plane[spot] = total

    load_ends.wait()
    load_count.wait()
    load_handed.wait()
    note[6:7] = jnp.full((1, LANES), scalars[0, 0], jnp.int32)
    note[7:8] = jnp.full((1, LANES), scalars[1, 0], jnp.int32)

    pl.semaphore_wait(
        barrier,
        NG * (NY - y) - 1 + jnp.where(y > 0, NZ - 1, NZ - 1 - z) + jnp.minimum(NSHARDS - 1 - shard, 2))

    spreads = []
    for dy in range(NY):
        for dg in range(NG):
            if dy or dg:
                spreads.append((dy, pltpu.make_async_remote_copy(
                    src_ref=mine.at[0], dst_ref=plane.at[spot],
                    send_sem=p1_send.at[dy * NG + dg], recv_sem=p1_recv.at[dy * NG + dg],
                    device_id=plane_device(dy, dg), device_id_type=MESH)))

    def plane_all(valid, act):
        for dy in range(NY):
            @pl.when(valid(dy))
            def _():
                for at, copy in spreads:
                    if at == dy:
                        act(copy)

    plane_all(lambda dy: y + dy < NY, lambda copy: copy.start())

    pass_codes = pltpu.make_async_remote_copy(
        src_ref=own, dst_ref=prev, send_sem=pass_send.at[0], recv_sem=pass_recv.at[0],
        device_id=device_of(jnp.minimum(shard + 1, NSHARDS - 1)), device_id_type=MESH)
    pass_note = pltpu.make_async_remote_copy(
        src_ref=note, dst_ref=got, send_sem=pass_send.at[1], recv_sem=pass_recv.at[1],
        device_id=device_of(jnp.minimum(shard + 1, NSHARDS - 1)), device_id_type=MESH)
    pass_tail = pltpu.make_async_remote_copy(
        src_ref=own.at[pl.ds(ROWS // 2, ROWS // 2)], dst_ref=prior, send_sem=pass_send.at[2], recv_sem=pass_recv.at[2],
        device_id=device_of(jnp.minimum(shard + 2, NSHARDS - 1)), device_id_type=MESH)

    @pl.when(shard + 1 < NSHARDS)
    def _():
        pass_note.start()
        pass_codes.start()

    @pl.when(shard + 2 < NSHARDS)
    def _():
        pass_tail.start()

    plane_all(lambda dy: y >= dy, lambda copy: copy.wait_recv())

    below = jnp.zeros((1, CODES), F32)
    level = jnp.zeros((1, CODES), F32)
    inside = jnp.zeros((1, CODES), F32)
    for k in range(PLANE):
        part = plane[k]
        below = below + jnp.where(k // NG < y, part, 0.0)
        here = jnp.where(k // NG == y, part, 0.0)
        level = level + here
        inside = inside + jnp.where(k % NG < grp, here, 0.0)
    sums[0] = below
    sums[1] = below + level

    climbs = []
    for k in range(1, NZ):
        after = ((z + k) % NZ > z).astype(jnp.int32)
        climbs.append(pltpu.make_async_remote_copy(
            src_ref=sums.at[after], dst_ref=column.at[z], send_sem=p2_send.at[k], recv_sem=p2_recv.at[k],
            device_id=column_device(k), device_id_type=MESH))
    for k, climb in enumerate(climbs, 1):
        pl.when(climbs_to(k))(climb.start)
    column[z] = below + inside

    @pl.when(shard >= 1)
    def _():
        pass_note.wait_recv()
        pass_codes.wait_recv()

    inner = grp > 0
    arrived = jnp.where(inner, got[7:8], 0)
    arrived = jnp.concatenate([arrived, arrived], axis=1)
    behind = jnp.concatenate([got[6:7], got[6:7]], axis=1) - arrived
    kept = note[6:7] - note[7:8]
    kept = jnp.concatenate([kept, kept], axis=1)
    own_line = ends_line(note[...], CAP, SHARD // 256)
    got_line = jnp.where(inner, ends_line(got[...], SLOTS, 0).astype(F32), 0.0).astype(BF16)
    lane = lax.broadcasted_iota(jnp.int32, (1, HAND), 1)
    block_of = block_column()

    known = jnp.where(shard >= 1, prev[...], -1)
    spread = enter(1, known[0:32]) + enter(2, known[32:64])
    before = dot_nt(jnp.ones((8, LANES), BF16), spread)[0:1]

    @pl.when(shard >= 2)
    def _():
        pass_tail.wait_recv()

    enter(0, jnp.where(shard >= 2, prior[...], -1))

    for part in range(2):
        ends = dot(own_line[:, : HAND * (part + 1)], picks(HAND * (part + 1), -arrived, HAND * part))
        if part == 0:
            ends = ends + dot(got_line, picks(SLOTS, behind, 0))
        ends = (ends[0:1] * 256.0 + ends[1:2]).astype(jnp.int32)
        valid = lane + HAND * part - arrived < kept
        upto = (ends + ((shard - 1) * SHARD + 1)).astype(F32)
        inv = jnp.where(valid, 256.0 / upto, 0.0)
        scale = jnp.where(valid, 256.0 / jnp.minimum(upto, float(WINDOW)), 0.0)
        key = ends // BLOCK
        halves = range(1 + 2 * part, 5)
        left, right = HALF_BLOCKS * halves[0], HALF_BLOCKS * 5
        less, same = [], []
        for half in halves:
            there = tall(key - HALF_BLOCKS * (half - 1), HALF_BLOCKS)
            less.append(flag(block_of < there))
            same.append(flag(block_of == there))
        less, same = jnp.concatenate(less, axis=0), jnp.concatenate(same, axis=0)
        upper = dot(counts[:, left:right], less)
        lower = dot(counts[:, left - HALF_BLOCKS : right - HALF_BLOCKS], less)
        tail = dot(counts[:, left - HALF_BLOCKS : left], jnp.ones((HALF_BLOCKS, LANES), BF16))
        found = jnp.concatenate(
            [blocks[:, left:right], blocks[:, left - HALF_BLOCKS : right - HALF_BLOCKS]], axis=0)
        found = dot(found, same)
        place = lax.broadcasted_iota(jnp.int32, (2 * BLOCK, HAND), 0) % BLOCK
        found = jnp.where(place <= ends % BLOCK, found, -1.0)
        for side in range(2):
            at = slice(side * LANES, (side + 1) * LANES)
            high = upper[:, at] + block_counts(found[:BLOCK, at]).astype(F32)
            low = lower[:, at] + block_counts(found[BLOCK:, at]).astype(F32)
            share = (high + tail - low) * scale[:, at]
            gap = share - high * inv[:, at]
            rows = pl.ds(HAND * part + LANES * side, LANES)
            share_ref[rows] = jnp.transpose(share)
            gap_ref[rows] = jnp.transpose(gap)
            inv_ref[rows] = jnp.transpose(jnp.broadcast_to(inv[:, at], (LANES, LANES)))

    for k, climb in enumerate(climbs, 1):
        pl.when(climbs_from(k))(climb.wait_recv)
    offset = jnp.zeros((1, CODES), F32)
    for k in range(NZ):
        used = jnp.logical_or(y > 0, k <= z)
        offset = offset + jnp.where(used, column[k], 0.0)
    off_ref[0:1] = offset - before
    off_ref[1:2] = offset

    plane_all(lambda dy: y + dy < NY, lambda copy: copy.wait_send())
    for k, climb in enumerate(climbs, 1):
        pl.when(climbs_to(k))(climb.wait_send)

    @pl.when(shard + 1 < NSHARDS)
    def _():
        pass_note.wait_send()
        pass_codes.wait_send()

    @pl.when(shard + 2 < NSHARDS)
    def _():
        pass_tail.wait_send()


def place_kernel(share_ref, gap_ref, inv_ref, off_ref, share_hbm, gap_hbm, buf, sem):
    share = pltpu.make_async_copy(share_ref, share_hbm, sem.at[0])
    share.start()
    n = LANES
    copies = [share]
    for i in range(CAP // n):
        at = pl.ds(i * n, n)
        inv = inv_ref[at]
        offset = off_ref[0:1] if i * n < HAND else off_ref[1:2]
        buf[at] = gap_ref[at] - jnp.concatenate([inv, inv], axis=1) * offset
        copies.append(pltpu.make_async_copy(buf.at[at], gap_hbm.at[at], sem.at[1 + i]))
        copies[-1].start()
    for copy in copies:
        copy.wait()


def local(event_codes, window_ends, window_count, handed):
    vmem = pl.BlockSpec(memory_space=pltpu.VMEM)
    hbm = pl.BlockSpec(memory_space=pl.ANY)
    far = pl.BlockSpec(memory_space=pltpu.HBM)
    dma = pltpu.SemaphoreType.DMA

    def stay(array):
        return pltpu.with_memory_space_constraint(array, pltpu.HBM)

    tallies = pl.pallas_call(
        tally_kernel,
        out_shape=(
            jax.ShapeDtypeStruct((CAP, CODES), F32),
            jax.ShapeDtypeStruct((CAP, CODES), F32),
            jax.ShapeDtypeStruct((CAP, LANES), F32),
            jax.ShapeDtypeStruct((8, CODES), F32),
        ),
        in_specs=[far] * 4,
        out_specs=(vmem,) * 4,
        scratch_shapes=[
            pltpu.VMEM((ROWS, LANES), jnp.int32),
            pltpu.VMEM((ROWS, LANES), jnp.int32),
            pltpu.VMEM((ROWS // 2, LANES), jnp.int32),
            pltpu.VMEM((8, LANES), jnp.int32),
            pltpu.VMEM((8, LANES), jnp.int32),
            pltpu.VMEM((1, 1, CODES), F32),
            pltpu.VMEM((PLANE, 1, CODES), F32),
            pltpu.VMEM((2, 1, CODES), F32),
            pltpu.VMEM((NZ, 1, CODES), F32),
            pltpu.VMEM((CODES, 5 * HALF_BLOCKS), BF16),
            pltpu.VMEM((BLOCK, 5 * HALF_BLOCKS), BF16),
            pltpu.SMEM((2, 1), jnp.int32),
            dma((4,)), dma((PLANE,)), dma((PLANE,)), dma((NZ,)), dma((NZ,)), dma((3,)), dma((3,)),
        ],
        compiler_params=pltpu.CompilerParams(
            collective_id=0, has_side_effects=True, vmem_limit_bytes=32 * 2**20),
        name="tally",
    )(stay(event_codes.reshape(ROWS, LANES)), stay(window_ends.reshape(SLOTS // LANES, LANES)), window_count, handed)
    return pl.pallas_call(
        place_kernel,
        out_shape=(jax.ShapeDtypeStruct((CAP, CODES), F32),) * 2,
        in_specs=[vmem] * 4,
        out_specs=(hbm, hbm),
        scratch_shapes=[pltpu.VMEM((CAP, CODES), F32), dma((1 + CAP // LANES,))],
        compiler_params=pltpu.CompilerParams(vmem_limit_bytes=16 * 2**20),
        name="place",
    )(*tallies)


def solution(mesh):
    both = ("seq", "grp")
    return jax.shard_map(
        local,
        mesh=mesh,
        in_specs=(P(both), P(both), P(both), P(both)),
        out_specs=(P(both, None), P(both, None)),
        check_vma=False,
    )
```

time: 27.7 us -> 21.9 us (0.79)
  the two profiles are of different devices: /device:TPU:1 before, /device:TPU:24 now
where the time goes in v2:
time: 21.9 us; the launch traced here: 21.7 us
  Pallas kernels  19.8 us (90%)
  between operations  1.93 us (9%)
    pallas_call x1, Pallas kernels, local(): pl.pallas_call(tally_kernel, out_shape=(jax.ShapeDtypeStruct((CAP, CODES)...  18.8 us
    pallas_call x1, Pallas kernels, local(): pl.pallas_call(place_kernel, out_shape=(jax.ShapeDtypeStruct((CAP, CODES)...  1 us

profile of v2, /device:TPU:24, one launch (start us, length us, event | category | flops | bytes accessed | tf_op | source)
XLA Modules:
  0.0 21.7 jit_solution(1778931487892718516)
XLA Ops:
  1.9 18.8 %tally.1 = (f32[512,256]{1,0:T(8,128)S(1)}, f32[512,256]{1,0:T(8,128)S(1)}, f32[512,128]{1,0:T(8,128)S(1)}, f32[8,256]{1,0:T(8,128)S(1)}) custom-call(s32[64,128]{1,0:T(8,128)} %bitcast.2, s32[6,128]{1,0:T(8,128)} %bitcast.3, s32[1]{0:T(128)S(6)} %copy.6.count_hbm, s32[1]{0:T(128)S(6)} %copy.7.handed_hbm), custom_call_target="tpu_custom_call" | custom-call | tf_op jit(solution)/shard_map/tally/pallas_call | solution.py:336
  20.7 1.0 %place.1 = (f32[512,256]{1,0:T(8,128)}, f32[512,256]{1,0:T(8,128)}) custom-call(f32[512,256]{1,0:T(8,128)S(1)} %get-tuple-element.6.share_ref, f32[512,256]{1,0:T(8,128)S(1)} %get-tuple-element.7.gap_ref, f32[512,128]{1,0:T(8,128)S(1)} %get-tuple-element.8.inv_ref, f32[8,256]{1,0:T(8,128)S(1)} %get-tuple-element.9.off_ref), custom_call_target="tpu_custom_call" | custom-call | tf_op jit(solution)/shard_map/place/pallas_call | solution.py:365

commit v3 on v2

--- a/solution.py
+++ b/solution.py
@@ -15,6 +15,7 @@
 HAND = CAP // 2
 NY, NZ, NG = 4, 8, 8
 PLANE = NY * NG
+HUB = 1
 NSHARDS = NY * NZ * NG
 LANES = 128
 ROWS = SHARD // LANES
@@ -27,7 +28,7 @@
 
 
 def device_of(shard):
-    return (shard // NG, shard % NG)
+    return (lax.div(shard, NG), lax.rem(shard, NG))
 
 
 def one_hot(row):
@@ -87,52 +88,50 @@
 
 
 def tally_kernel(
-    codes_hbm, ends_hbm, count_hbm, handed_hbm,
+    codes_hbm, ends_hbm, handed_hbm,
     share_ref, gap_ref, inv_ref, off_ref,
     own, prev, prior, note, got, mine, plane, sums, column, counts, blocks, scalars,
     load_sem, p1_send, p1_recv, p2_send, p2_recv, pass_send, pass_recv,
 ):
     seq, grp = lax.axis_index("seq"), lax.axis_index("grp")
-    y, z = seq // NZ, seq % NZ
+    y, z = lax.div(seq, NZ), lax.rem(seq, NZ)
     shard = seq * NG + grp
     spot = y * NG + grp
+    hub = grp == HUB
 
     load_codes = pltpu.make_async_copy(codes_hbm, own, load_sem.at[0])
     load_ends = pltpu.make_async_copy(ends_hbm, note.at[pl.ds(0, 6)], load_sem.at[1])
-    load_count = pltpu.make_async_copy(count_hbm, scalars.at[0], load_sem.at[2])
-    load_handed = pltpu.make_async_copy(handed_hbm, scalars.at[1], load_sem.at[3])
+    load_handed = pltpu.make_async_copy(handed_hbm, scalars, load_sem.at[2])
     load_codes.start()
     load_ends.start()
-    load_count.start()
     load_handed.start()
 
     barrier = pltpu.get_barrier_semaphore()
 
-    def plane_device(dy, dg):
-        return ((y + dy) * NZ + z, (grp + dg + NG) % NG)
-
-    def column_device(k):
-        return (y * NZ + (z + k + NZ) % NZ, grp)
-
-    def climbs_to(k):
-        return jnp.logical_or(y > 0, (z + k) % NZ > z)
-
-    def climbs_from(k):
-        return jnp.logical_or(y > 0, (z - k + NZ) % NZ < z)
-
-    def greet(device):
-        pl.semaphore_signal(barrier, inc=1, device_id=device, device_id_type=MESH)
-
-    for dy in range(NY):
-        @pl.when(y >= dy)
-        def _():
-            for dg in range(NG):
-                if dy or dg:
-                    greet(plane_device(-dy, -dg))
-    for k in range(1, NZ):
-        pl.when(climbs_from(k))(functools.partial(greet, column_device(-k)))
+    def greet(row, group):
+        pl.semaphore_signal(barrier, inc=1, device_id=(row, group), device_id_type=MESH)
+
+    def feeds(z2):
+        return jnp.logical_or(z2 < z, jnp.logical_and(y > 0, z2 != z))
+
+    def fed(z2):
+        return jnp.logical_or(z2 > z, jnp.logical_and(y > 0, z2 != z))
+
+    for g2 in range(NG):
+        pl.when(grp != g2)(functools.partial(greet, seq, g2))
+    for z2 in range(NZ):
+        pl.when(feeds(z2))(functools.partial(greet, y * NZ + z2, HUB))
+
+    @pl.when(hub)
+    def _():
+        for y2 in range(NY - 1):
+            @pl.when(y2 < y)
+            def _():
+                for g2 in range(NG):
+                    greet(y2 * NZ + z, g2)
+
     for back in (1, 2):
-        pl.when(shard >= back)(functools.partial(greet, device_of(shard - back)))
+        pl.when(shard >= back)(functools.partial(greet, *device_of(shard - back)))
 
     def enter(half, codes):
         by = by_block(codes)
@@ -151,33 +150,26 @@
     plane[spot] = total
 
     load_ends.wait()
-    load_count.wait()
     load_handed.wait()
-    note[6:7] = jnp.full((1, LANES), scalars[0, 0], jnp.int32)
-    note[7:8] = jnp.full((1, LANES), scalars[1, 0], jnp.int32)
-
-    pl.semaphore_wait(
-        barrier,
-        NG * (NY - y) - 1 + jnp.where(y > 0, NZ - 1, NZ - 1 - z) + jnp.minimum(NSHARDS - 1 - shard, 2))
-
-    spreads = []
-    for dy in range(NY):
-        for dg in range(NG):
-            if dy or dg:
-                spreads.append((dy, pltpu.make_async_remote_copy(
-                    src_ref=mine.at[0], dst_ref=plane.at[spot],
-                    send_sem=p1_send.at[dy * NG + dg], recv_sem=p1_recv.at[dy * NG + dg],
-                    device_id=plane_device(dy, dg), device_id_type=MESH)))
-
-    def plane_all(valid, act):
-        for dy in range(NY):
-            @pl.when(valid(dy))
-            def _():
-                for at, copy in spreads:
-                    if at == dy:
-                        act(copy)
-
-    plane_all(lambda dy: y + dy < NY, lambda copy: copy.start())
+    slots = jnp.sum((note[0:6] > 0).astype(F32), axis=0, keepdims=True)
+    slots = jnp.sum(slots, axis=1, keepdims=True) + (note[0:1, 0:1] == 0).astype(F32)
+    note[6:7] = jnp.broadcast_to(slots.astype(jnp.int32), (1, LANES))
+    note[7:8] = jnp.full((1, LANES), scalars[0], jnp.int32)
+
+    columns = jnp.where(hub, NG * jnp.where(y > 0, NZ - 1, NZ - 1 - z), 0)
+    pl.semaphore_wait(barrier, NG - 1 + NY - 1 - y + columns + jnp.minimum(NSHARDS - 1 - shard, 2))
+
+    def spread_to(row, group, sem, source):
+        return pltpu.make_async_remote_copy(
+            src_ref=mine.at[0], dst_ref=plane.at[source], send_sem=p1_send.at[sem], recv_sem=p1_recv.at[source],
+            device_id=(row, group), device_id_type=MESH)
+
+    to_hubs = [(y2, spread_to(y2 * NZ + z, HUB, NG + y2, spot)) for y2 in range(1, NY)]
+    to_mates = [(g2, spread_to(seq, g2, g2, spot)) for g2 in (HUB, 0, 2, 3, 4, 5, 6, 7)]
+    for y2, copy in to_hubs:
+        pl.when(y2 > y)(copy.start)
+    for g2, copy in to_mates:
+        pl.when(grp != g2)(copy.start)
 
     pass_codes = pltpu.make_async_remote_copy(
         src_ref=own, dst_ref=prev, send_sem=pass_send.at[0], recv_sem=pass_recv.at[0],
@@ -198,29 +190,49 @@
     def _():
         pass_tail.start()
 
-    plane_all(lambda dy: y >= dy, lambda copy: copy.wait_recv())
-
-    below = jnp.zeros((1, CODES), F32)
-    level = jnp.zeros((1, CODES), F32)
-    inside = jnp.zeros((1, CODES), F32)
-    for k in range(PLANE):
-        part = plane[k]
-        below = below + jnp.where(k // NG < y, part, 0.0)
-        here = jnp.where(k // NG == y, part, 0.0)
-        level = level + here
-        inside = inside + jnp.where(k % NG < grp, here, 0.0)
-    sums[0] = below
-    sums[1] = below + level
+    def hear_mates():
+        for g2 in range(NG):
+            pl.when(grp != g2)(spread_to(seq, g2, g2, y * NG + g2).wait_recv)
 
     climbs = []
-    for k in range(1, NZ):
-        after = ((z + k) % NZ > z).astype(jnp.int32)
-        climbs.append(pltpu.make_async_remote_copy(
-            src_ref=sums.at[after], dst_ref=column.at[z], send_sem=p2_send.at[k], recv_sem=p2_recv.at[k],
-            device_id=column_device(k), device_id_type=MESH))
-    for k, climb in enumerate(climbs, 1):
-        pl.when(climbs_to(k))(climb.start)
-    column[z] = below + inside
+    for z2 in range(NZ):
+        for g2 in range(NG):
+            climbs.append((z2, g2, pltpu.make_async_remote_copy(
+                src_ref=sums.at[(z2 > z).astype(jnp.int32)], dst_ref=column.at[z],
+                send_sem=p2_send.at[z2 * NG + g2], recv_sem=p2_recv.at[z],
+                device_id=(y * NZ + z2, g2), device_id_type=MESH)))
+
+    def climb_all(act):
+        for z2 in range(NZ):
+            @pl.when(fed(z2))
+            def _():
+                for at, g2, copy in climbs:
+                    if at == z2:
+                        act(copy)
+            @pl.when(jnp.logical_and(z2 == z, y > 0))
+            def _():
+                for at, g2, copy in climbs:
+                    if at == z2 and g2 != HUB:
+                        act(copy)
+
+    @pl.when(hub)
+    def _():
+        below = jnp.zeros((1, CODES), F32)
+        level = jnp.zeros((1, CODES), F32)
+        hear_mates()
+        for g2 in range(NG):
+            level = level + plane[y * NG + g2]
+        for y2 in range(NY - 1):
+            @pl.when(y2 < y)
+            def _():
+                for g2 in range(NG):
+                    spread_to(seq, g2, g2, y2 * NG + g2).wait_recv()
+            for g2 in range(NG):
+                below = below + jnp.where(y2 < y, plane[y2 * NG + g2], 0.0)
+        sums[0] = below
+        sums[1] = below + level
+        column[z] = below
+        climb_all(lambda copy: copy.start())
 
     @pl.when(shard >= 1)
     def _():
@@ -285,18 +297,30 @@
             gap_ref[rows] = jnp.transpose(gap)
             inv_ref[rows] = jnp.transpose(jnp.broadcast_to(inv[:, at], (LANES, LANES)))
 
-    for k, climb in enumerate(climbs, 1):
-        pl.when(climbs_from(k))(climb.wait_recv)
-    offset = jnp.zeros((1, CODES), F32)
-    for k in range(NZ):
-        used = jnp.logical_or(y > 0, k <= z)
-        offset = offset + jnp.where(used, column[k], 0.0)
+    pl.when(jnp.logical_not(hub))(hear_mates)
+    inside = jnp.zeros((1, CODES), F32)
+    for g2 in range(NG - 1):
+        inside = inside + jnp.where(g2 < grp, plane[y * NG + g2], 0.0)
+
+    def hear_column(z2):
+        pltpu.make_async_remote_copy(
+            src_ref=sums.at[0], dst_ref=column.at[z2], send_sem=p2_send.at[z2], recv_sem=p2_recv.at[z2],
+            device_id=(y * NZ + z2, HUB), device_id_type=MESH).wait_recv()
+
+    offset = inside
+    for z2 in range(NZ):
+        pl.when(jnp.logical_or(feeds(z2), jnp.logical_and(jnp.logical_not(hub), jnp.logical_and(z2 == z, y > 0))))(
+            functools.partial(hear_column, z2))
+    for z2 in range(NZ):
+        offset = offset + jnp.where(jnp.logical_or(z2 < z, y > 0), column[z2], 0.0)
     off_ref[0:1] = offset - before
     off_ref[1:2] = offset
 
-    plane_all(lambda dy: y + dy < NY, lambda copy: copy.wait_send())
-    for k, climb in enumerate(climbs, 1):
-        pl.when(climbs_to(k))(climb.wait_send)
+    for y2, copy in to_hubs:
+        pl.when(y2 > y)(copy.wait_send)
+    for g2, copy in to_mates:
+        pl.when(grp != g2)(copy.wait_send)
+    pl.when(hub)(functools.partial(climb_all, lambda copy: copy.wait_send()))
 
     @pl.when(shard + 1 < NSHARDS)
     def _():
@@ -341,7 +365,7 @@
             jax.ShapeDtypeStruct((CAP, LANES), F32),
             jax.ShapeDtypeStruct((8, CODES), F32),
         ),
-        in_specs=[far] * 4,
+        in_specs=[far] * 3,
         out_specs=(vmem,) * 4,
         scratch_shapes=[
             pltpu.VMEM((ROWS, LANES), jnp.int32),
@@ -355,13 +379,13 @@
             pltpu.VMEM((NZ, 1, CODES), F32),
             pltpu.VMEM((CODES, 5 * HALF_BLOCKS), BF16),
             pltpu.VMEM((BLOCK, 5 * HALF_BLOCKS), BF16),
-            pltpu.SMEM((2, 1), jnp.int32),
-            dma((4,)), dma((PLANE,)), dma((PLANE,)), dma((NZ,)), dma((NZ,)), dma((3,)), dma((3,)),
+            pltpu.SMEM((1,), jnp.int32),
+            dma((3,)), dma((NG + NY,)), dma((PLANE,)), dma((NZ * NG,)), dma((NZ,)), dma((3,)), dma((3,)),
         ],
         compiler_params=pltpu.CompilerParams(
             collective_id=0, has_side_effects=True, vmem_limit_bytes=32 * 2**20),
         name="tally",
-    )(stay(event_codes.reshape(ROWS, LANES)), stay(window_ends.reshape(SLOTS // LANES, LANES)), window_count, handed)
+    )(stay(event_codes.reshape(ROWS, LANES)), stay(window_ends.reshape(SLOTS // LANES, LANES)), handed)
     return pl.pallas_call(
         place_kernel,
         out_shape=(jax.ShapeDtypeStruct((CAP, CODES), F32),) * 2,

time: 21.9 us -> 19.6 us (0.89)
  the two profiles are of different devices: /device:TPU:24 before, /device:TPU:9 now
where the time goes in v3:
time: 19.6 us; the launch traced here: 19.5 us
  Pallas kernels  18.2 us (93%)
  between operations  1.28 us (7%)
    pallas_call x1, Pallas kernels, local(): pl.pallas_call(tally_kernel, out_shape=(jax.ShapeDtypeStruct((CAP, CODES)...  17.2 us
    pallas_call x1, Pallas kernels, local(): pl.pallas_call(place_kernel, out_shape=(jax.ShapeDtypeStruct((CAP, CODES)...  1 us

profile of v3, /device:TPU:9, one launch (start us, length us, event | category | flops | bytes accessed | tf_op | source)
XLA Modules:
  0.0 19.5 jit_solution(9162337519507676254)
XLA Ops:
  1.3 17.2 %tally.1 = (f32[512,256]{1,0:T(8,128)S(1)}, f32[512,256]{1,0:T(8,128)S(1)}, f32[512,128]{1,0:T(8,128)S(1)}, f32[8,256]{1,0:T(8,128)S(1)}) custom-call(s32[64,128]{1,0:T(8,128)} %bitcast.2, s32[6,128]{1,0:T(8,128)} %bitcast.3, s32[1]{0:T(128)S(6)} %copy.5.handed_hbm), custom_call_target="tpu_custom_call" | custom-call | tf_op jit(solution)/shard_map/tally/pallas_call | solution.py:360
  18.5 1.0 %place.1 = (f32[512,256]{1,0:T(8,128)}, f32[512,256]{1,0:T(8,128)}) custom-call(f32[512,256]{1,0:T(8,128)S(1)} %get-tuple-element.6.share_ref, f32[512,256]{1,0:T(8,128)S(1)} %get-tuple-element.7.gap_ref, f32[512,128]{1,0:T(8,128)S(1)} %get-tuple-element.8.inv_ref, f32[8,256]{1,0:T(8,128)S(1)} %get-tuple-element.9.off_ref), custom_call_target="tpu_custom_call" | custom-call | tf_op jit(solution)/shard_map/place/pallas_call | solution.py:389

commit v4 on v3

--- a/solution.py
+++ b/solution.py
@@ -99,10 +99,13 @@
     spot = y * NG + grp
     hub = grp == HUB
 
-    load_codes = pltpu.make_async_copy(codes_hbm, own, load_sem.at[0])
-    load_ends = pltpu.make_async_copy(ends_hbm, note.at[pl.ds(0, 6)], load_sem.at[1])
-    load_handed = pltpu.make_async_copy(handed_hbm, scalars, load_sem.at[2])
-    load_codes.start()
+    load_codes = [
+        pltpu.make_async_copy(codes_hbm.at[pl.ds(i * BLOCK, BLOCK)], own.at[pl.ds(i * BLOCK, BLOCK)], load_sem.at[2 + i])
+        for i in range(ROWS // BLOCK)]
+    load_ends = pltpu.make_async_copy(ends_hbm, note.at[pl.ds(0, 6)], load_sem.at[0])
+    load_handed = pltpu.make_async_copy(handed_hbm, scalars, load_sem.at[1])
+    for load in load_codes:
+        load.start()
     load_ends.start()
     load_handed.start()
 
@@ -116,11 +119,6 @@
 
     def fed(z2):
         return jnp.logical_or(z2 > z, jnp.logical_and(y > 0, z2 != z))
-
-    for g2 in range(NG):
-        pl.when(grp != g2)(functools.partial(greet, seq, g2))
-    for z2 in range(NZ):
-        pl.when(feeds(z2))(functools.partial(greet, y * NZ + z2, HUB))
 
     @pl.when(hub)
     def _():
@@ -129,6 +127,11 @@
             def _():
                 for g2 in range(NG):
                     greet(y2 * NZ + z, g2)
+
+    for g2 in range(NG):
+        pl.when(grp != g2)(functools.partial(greet, seq, g2))
+    for z2 in range(NZ):
+        pl.when(feeds(z2))(functools.partial(greet, y * NZ + z2, HUB))
 
     for back in (1, 2):
         pl.when(shard >= back)(functools.partial(greet, *device_of(shard - back)))
@@ -143,8 +146,10 @@
         blocks[:, at + LANES : at + HALF_BLOCKS] = by[BLOCK:].astype(BF16)
         return first + second
 
-    load_codes.wait()
-    spread = enter(3, own[0:32]) + enter(4, own[32:64])
+    spread = jnp.zeros((CODES, LANES), BF16)
+    for i, load in enumerate(load_codes):
+        load.wait()
+        spread = spread + block_counts(own[i * BLOCK : (i + 1) * BLOCK].astype(F32))
     total = dot_nt(jnp.ones((8, LANES), BF16), spread)[0:1]
     mine[0] = total
     plane[spot] = total
@@ -159,13 +164,18 @@
     columns = jnp.where(hub, NG * jnp.where(y > 0, NZ - 1, NZ - 1 - z), 0)
     pl.semaphore_wait(barrier, NG - 1 + NY - 1 - y + columns + jnp.minimum(NSHARDS - 1 - shard, 2))
 
-    def spread_to(row, group, sem, source):
+    def spread_to(row, group, sem, batch):
         return pltpu.make_async_remote_copy(
-            src_ref=mine.at[0], dst_ref=plane.at[source], send_sem=p1_send.at[sem], recv_sem=p1_recv.at[source],
+            src_ref=mine.at[0], dst_ref=plane.at[spot], send_sem=p1_send.at[sem], recv_sem=p1_recv.at[batch],
             device_id=(row, group), device_id_type=MESH)
 
-    to_hubs = [(y2, spread_to(y2 * NZ + z, HUB, NG + y2, spot)) for y2 in range(1, NY)]
-    to_mates = [(g2, spread_to(seq, g2, g2, spot)) for g2 in (HUB, 0, 2, 3, 4, 5, 6, 7)]
+    def batch_of(n, send_sem, recv_sem):
+        return pltpu.make_async_remote_copy(
+            src_ref=plane.at[pl.ds(0, n)], dst_ref=plane.at[pl.ds(0, n)], send_sem=send_sem, recv_sem=recv_sem,
+            device_id=(seq, grp), device_id_type=MESH)
+
+    to_hubs = [(y2, spread_to(y2 * NZ + z, HUB, y2, y)) for y2 in range(1, NY)]
+    to_mates = [(g2, spread_to(seq, g2, 0, NY)) for g2 in (HUB, 0, 2, 3, 4, 5, 6, 7)]
     for y2, copy in to_hubs:
         pl.when(y2 > y)(copy.start)
     for g2, copy in to_mates:
@@ -190,16 +200,18 @@
     def _():
         pass_tail.start()
 
+    enter(3, own[0:32])
+    enter(4, own[32:64])
+
     def hear_mates():
-        for g2 in range(NG):
-            pl.when(grp != g2)(spread_to(seq, g2, g2, y * NG + g2).wait_recv)
+        batch_of(NG - 1, p1_send.at[0], p1_recv.at[NY]).wait_recv()
 
     climbs = []
     for z2 in range(NZ):
         for g2 in range(NG):
             climbs.append((z2, g2, pltpu.make_async_remote_copy(
                 src_ref=sums.at[(z2 > z).astype(jnp.int32)], dst_ref=column.at[z],
-                send_sem=p2_send.at[z2 * NG + g2], recv_sem=p2_recv.at[z],
+                send_sem=p2_send.at[z2], recv_sem=p2_recv.at[z],
                 device_id=(y * NZ + z2, g2), device_id_type=MESH)))
 
     def climb_all(act):
@@ -225,8 +237,7 @@
         for y2 in range(NY - 1):
             @pl.when(y2 < y)
             def _():
-                for g2 in range(NG):
-                    spread_to(seq, g2, g2, y2 * NG + g2).wait_recv()
+                batch_of(NG, p1_send.at[0], p1_recv.at[y2]).wait_recv()
             for g2 in range(NG):
                 below = below + jnp.where(y2 < y, plane[y2 * NG + g2], 0.0)
         sums[0] = below
@@ -302,6 +313,25 @@
     for g2 in range(NG - 1):
         inside = inside + jnp.where(g2 < grp, plane[y * NG + g2], 0.0)
 
+    for y2, copy in to_hubs:
+        pl.when(y2 > y)(copy.wait_send)
+    batch_of(NG - 1, p1_send.at[0], p1_recv.at[NY]).wait_send()
+
+    @pl.when(hub)
+    def _():
+        for z2 in range(NZ):
+            pl.when(fed(z2))(batch_of(NG, p2_send.at[z2], p1_recv.at[NY]).wait_send)
+            pl.when(jnp.logical_and(z2 == z, y > 0))(batch_of(NG - 1, p2_send.at[z2], p1_recv.at[NY]).wait_send)
+
+    @pl.when(shard + 1 < NSHARDS)
+    def _():
+        pass_note.wait_send()
+        pass_codes.wait_send()
+
+    @pl.when(shard + 2 < NSHARDS)
+    def _():
+        pass_tail.wait_send()
+
     def hear_column(z2):
         pltpu.make_async_remote_copy(
             src_ref=sums.at[0], dst_ref=column.at[z2], send_sem=p2_send.at[z2], recv_sem=p2_recv.at[z2],
@@ -315,21 +345,6 @@
         offset = offset + jnp.where(jnp.logical_or(z2 < z, y > 0), column[z2], 0.0)
     off_ref[0:1] = offset - before
     off_ref[1:2] = offset
-
-    for y2, copy in to_hubs:
-        pl.when(y2 > y)(copy.wait_send)
-    for g2, copy in to_mates:
-        pl.when(grp != g2)(copy.wait_send)
-    pl.when(hub)(functools.partial(climb_all, lambda copy: copy.wait_send()))
-
-    @pl.when(shard + 1 < NSHARDS)
-    def _():
-        pass_note.wait_send()
-        pass_codes.wait_send()
-
-    @pl.when(shard + 2 < NSHARDS)
-    def _():
-        pass_tail.wait_send()
 
 
 def place_kernel(share_ref, gap_ref, inv_ref, off_ref, share_hbm, gap_hbm, buf, sem):
@@ -380,7 +395,7 @@
             pltpu.VMEM((CODES, 5 * HALF_BLOCKS), BF16),
             pltpu.VMEM((BLOCK, 5 * HALF_BLOCKS), BF16),
             pltpu.SMEM((1,), jnp.int32),
-            dma((3,)), dma((NG + NY,)), dma((PLANE,)), dma((NZ * NG,)), dma((NZ,)), dma((3,)), dma((3,)),
+            dma((2 + ROWS // BLOCK,)), dma((NY,)), dma((NY + 1,)), dma((NZ,)), dma((NZ,)), dma((3,)), dma((3,)),
         ],
         compiler_params=pltpu.CompilerParams(
             collective_id=0, has_side_effects=True, vmem_limit_bytes=32 * 2**20),

time: 19.6 us -> 18.7 us (0.954); the launches traced: 19.5 us -> 18.3 us
  Pallas kernels: 18.2 us -> 17.1 us
    pallas_call x1, Pallas kernels: 17.2 us -> 16.1 us  [local(): pl.pallas_call(tally_kernel, out_shape=(jax.ShapeDtypeStruct((CAP, CODES)...]
where the time goes in v4:
time: 18.7 us; the launch traced here: 18.3 us
  Pallas kernels  17.1 us (91%)
  between operations  1.28 us (7%)
    pallas_call x1, Pallas kernels, local(): pl.pallas_call(tally_kernel, out_shape=(jax.ShapeDtypeStruct((CAP, CODES)...  16.1 us
    pallas_call x1, Pallas kernels, local(): pl.pallas_call(place_kernel, out_shape=(jax.ShapeDtypeStruct((CAP, CODES)...  1 us

profile of v4, /device:TPU:9, one launch (start us, length us, event | category | flops | bytes accessed | tf_op | source)
XLA Modules:
  0.0 18.3 jit_solution(804102428873308971)
XLA Ops:
  1.3 16.1 %tally.1 = (f32[512,256]{1,0:T(8,128)S(1)}, f32[512,256]{1,0:T(8,128)S(1)}, f32[512,128]{1,0:T(8,128)S(1)}, f32[8,256]{1,0:T(8,128)S(1)}) custom-call(s32[64,128]{1,0:T(8,128)} %bitcast.2, s32[6,128]{1,0:T(8,128)} %bitcast.3, s32[1]{0:T(128)S(6)} %copy.5.handed_hbm), custom_call_target="tpu_custom_call" | custom-call | tf_op jit(solution)/shard_map/tally/pallas_call | solution.py:375
  17.3 1.0 %place.1 = (f32[512,256]{1,0:T(8,128)}, f32[512,256]{1,0:T(8,128)}) custom-call(f32[512,256]{1,0:T(8,128)S(1)} %get-tuple-element.6.share_ref, f32[512,256]{1,0:T(8,128)S(1)} %get-tuple-element.7.gap_ref, f32[512,128]{1,0:T(8,128)S(1)} %get-tuple-element.8.inv_ref, f32[8,256]{1,0:T(8,128)S(1)} %get-tuple-element.9.off_ref), custom_call_target="tpu_custom_call" | custom-call | tf_op jit(solution)/shard_map/place/pallas_call | solution.py:404

commit v5 on v4

--- a/solution.py
+++ b/solution.py
@@ -20,6 +20,7 @@
 LANES = 128
 ROWS = SHARD // LANES
 BLOCK = 16
+PIECES = 1
 HALF_BLOCKS = SHARD // BLOCK // 2
 MESH = pl.DeviceIdType.MESH
 NT = (((1,), (1,)), ((), ()))
@@ -117,9 +118,6 @@
     def feeds(z2):
         return jnp.logical_or(z2 < z, jnp.logical_and(y > 0, z2 != z))
 
-    def fed(z2):
-        return jnp.logical_or(z2 > z, jnp.logical_and(y > 0, z2 != z))
-
     @pl.when(hub)
     def _():
         for y2 in range(NY - 1):
@@ -127,9 +125,11 @@
             def _():
                 for g2 in range(NG):
                     greet(y2 * NZ + z, g2)
-
-    for g2 in range(NG):
-        pl.when(grp != g2)(functools.partial(greet, seq, g2))
+        for g2 in range(NG):
+            if g2 != HUB:
+                greet(seq, g2)
+
+    pl.when(jnp.logical_not(hub))(functools.partial(greet, seq, HUB))
     for z2 in range(NZ):
         pl.when(feeds(z2))(functools.partial(greet, y * NZ + z2, HUB))
 
@@ -146,27 +146,30 @@
         blocks[:, at + LANES : at + HALF_BLOCKS] = by[BLOCK:].astype(BF16)
         return first + second
 
+    def write_note():
+        load_ends.wait()
+        load_handed.wait()
+        slots = jnp.sum((note[0:6] > 0).astype(F32), axis=0, keepdims=True)
+        slots = jnp.sum(slots, axis=1, keepdims=True) + (note[0:1, 0:1] == 0).astype(F32)
+        note[6:7] = jnp.broadcast_to(slots.astype(jnp.int32), (1, LANES))
+        note[7:8] = jnp.full((1, LANES), scalars[0], jnp.int32)
+
     spread = jnp.zeros((CODES, LANES), BF16)
     for i, load in enumerate(load_codes):
         load.wait()
+        if i + 1 == len(load_codes):
+            write_note()
         spread = spread + block_counts(own[i * BLOCK : (i + 1) * BLOCK].astype(F32))
     total = dot_nt(jnp.ones((8, LANES), BF16), spread)[0:1]
     mine[0] = total
     plane[spot] = total
 
-    load_ends.wait()
-    load_handed.wait()
-    slots = jnp.sum((note[0:6] > 0).astype(F32), axis=0, keepdims=True)
-    slots = jnp.sum(slots, axis=1, keepdims=True) + (note[0:1, 0:1] == 0).astype(F32)
-    note[6:7] = jnp.broadcast_to(slots.astype(jnp.int32), (1, LANES))
-    note[7:8] = jnp.full((1, LANES), scalars[0], jnp.int32)
-
     columns = jnp.where(hub, NG * jnp.where(y > 0, NZ - 1, NZ - 1 - z), 0)
-    pl.semaphore_wait(barrier, NG - 1 + NY - 1 - y + columns + jnp.minimum(NSHARDS - 1 - shard, 2))
-
-    def spread_to(row, group, sem, batch):
+    pl.semaphore_wait(barrier, jnp.where(hub, NG - 1 + NY - 1 - y, NY - y) + columns + jnp.minimum(NSHARDS - 1 - shard, 2))
+
+    def spread_to(row, group, batch):
         return pltpu.make_async_remote_copy(
-            src_ref=mine.at[0], dst_ref=plane.at[spot], send_sem=p1_send.at[sem], recv_sem=p1_recv.at[batch],
+            src_ref=mine.at[0], dst_ref=plane.at[spot], send_sem=p1_send.at[0], recv_sem=p1_recv.at[batch],
             device_id=(row, group), device_id_type=MESH)
 
     def batch_of(n, send_sem, recv_sem):
@@ -174,21 +177,18 @@
             src_ref=plane.at[pl.ds(0, n)], dst_ref=plane.at[pl.ds(0, n)], send_sem=send_sem, recv_sem=recv_sem,
             device_id=(seq, grp), device_id_type=MESH)
 
-    to_hubs = [(y2, spread_to(y2 * NZ + z, HUB, y2, y)) for y2 in range(1, NY)]
-    to_mates = [(g2, spread_to(seq, g2, 0, NY)) for g2 in (HUB, 0, 2, 3, 4, 5, 6, 7)]
+    to_hubs = [(y2, spread_to(y2 * NZ + z, HUB, y)) for y2 in range(NY)]
     for y2, copy in to_hubs:
-        pl.when(y2 > y)(copy.start)
-    for g2, copy in to_mates:
-        pl.when(grp != g2)(copy.start)
+        pl.when(jnp.logical_or(y2 > y, jnp.logical_and(y2 == y, jnp.logical_not(hub))))(copy.start)
 
     pass_codes = pltpu.make_async_remote_copy(
         src_ref=own, dst_ref=prev, send_sem=pass_send.at[0], recv_sem=pass_recv.at[0],
         device_id=device_of(jnp.minimum(shard + 1, NSHARDS - 1)), device_id_type=MESH)
     pass_note = pltpu.make_async_remote_copy(
-        src_ref=note, dst_ref=got, send_sem=pass_send.at[1], recv_sem=pass_recv.at[1],
+        src_ref=note, dst_ref=got, send_sem=pass_send.at[0], recv_sem=pass_recv.at[0],
         device_id=device_of(jnp.minimum(shard + 1, NSHARDS - 1)), device_id_type=MESH)
     pass_tail = pltpu.make_async_remote_copy(
-        src_ref=own.at[pl.ds(ROWS // 2, ROWS // 2)], dst_ref=prior, send_sem=pass_send.at[2], recv_sem=pass_recv.at[2],
+        src_ref=own.at[pl.ds(ROWS // 2, ROWS // 2)], dst_ref=prior, send_sem=pass_send.at[0], recv_sem=pass_recv.at[1],
         device_id=device_of(jnp.minimum(shard + 2, NSHARDS - 1)), device_id_type=MESH)
 
     @pl.when(shard + 1 < NSHARDS)
@@ -203,52 +203,46 @@
     enter(3, own[0:32])
     enter(4, own[32:64])
 
-    def hear_mates():
-        batch_of(NG - 1, p1_send.at[0], p1_recv.at[NY]).wait_recv()
-
-    climbs = []
-    for z2 in range(NZ):
-        for g2 in range(NG):
-            climbs.append((z2, g2, pltpu.make_async_remote_copy(
-                src_ref=sums.at[(z2 > z).astype(jnp.int32)], dst_ref=column.at[z],
-                send_sem=p2_send.at[z2], recv_sem=p2_recv.at[z],
-                device_id=(y * NZ + z2, g2), device_id_type=MESH)))
-
-    def climb_all(act):
-        for z2 in range(NZ):
-            @pl.when(fed(z2))
-            def _():
-                for at, g2, copy in climbs:
-                    if at == z2:
-                        act(copy)
-            @pl.when(jnp.logical_and(z2 == z, y > 0))
-            def _():
-                for at, g2, copy in climbs:
-                    if at == z2 and g2 != HUB:
-                        act(copy)
+    def climb(z2, g2, kind):
+        pltpu.make_async_remote_copy(
+            src_ref=sums.at[kind], dst_ref=column.at[z], send_sem=p2_send.at[0], recv_sem=p2_recv.at[0],
+            device_id=(y * NZ + z2, g2), device_id_type=MESH).start()
 
     @pl.when(hub)
     def _():
-        below = jnp.zeros((1, CODES), F32)
-        level = jnp.zeros((1, CODES), F32)
-        hear_mates()
-        for g2 in range(NG):
-            level = level + plane[y * NG + g2]
+        sums[NG + 1] = jnp.zeros((1, CODES), F32)
         for y2 in range(NY - 1):
             @pl.when(y2 < y)
             def _():
                 batch_of(NG, p1_send.at[0], p1_recv.at[y2]).wait_recv()
-            for g2 in range(NG):
-                below = below + jnp.where(y2 < y, plane[y2 * NG + g2], 0.0)
-        sums[0] = below
-        sums[1] = below + level
-        column[z] = below
-        climb_all(lambda copy: copy.start())
+                part = sums[NG + 1]
+                for g2 in range(NG):
+                    part = part + plane[y2 * NG + g2]
+                sums[NG + 1] = part
+        for z2 in range(NZ - 1):
+            @pl.when(jnp.logical_and(y > 0, z2 < z))
+            def _():
+                for g2 in range(NG):
+                    climb(z2, g2, NG + 1)
+        batch_of(NG - 1, p1_send.at[0], p1_recv.at[y]).wait_recv()
+        below = sums[NG + 1]
+        for g2 in range(NG):
+            sums[g2] = below
+            below = below + plane[y * NG + g2]
+        sums[NG] = below
+        for z2 in range(1, NZ):
+            @pl.when(z2 > z)
+            def _():
+                for g2 in range(NG):
+                    climb(z2, g2, NG)
+        for g2 in range(NG):
+            if g2 != HUB:
+                climb(z, g2, g2)
+        column[z] = sums[HUB]
 
     @pl.when(shard >= 1)
     def _():
-        pass_note.wait_recv()
-        pass_codes.wait_recv()
+        batch_of(4 + 32, p1_send.at[0], pass_recv.at[0]).wait_recv()
 
     inner = grp > 0
     arrived = jnp.where(inner, got[7:8], 0)
@@ -308,41 +302,43 @@
             gap_ref[rows] = jnp.transpose(gap)
             inv_ref[rows] = jnp.transpose(jnp.broadcast_to(inv[:, at], (LANES, LANES)))
 
-    pl.when(jnp.logical_not(hub))(hear_mates)
-    inside = jnp.zeros((1, CODES), F32)
-    for g2 in range(NG - 1):
-        inside = inside + jnp.where(g2 < grp, plane[y * NG + g2], 0.0)
-
-    for y2, copy in to_hubs:
-        pl.when(y2 > y)(copy.wait_send)
-    batch_of(NG - 1, p1_send.at[0], p1_recv.at[NY]).wait_send()
-
-    @pl.when(hub)
-    def _():
-        for z2 in range(NZ):
-            pl.when(fed(z2))(batch_of(NG, p2_send.at[z2], p1_recv.at[NY]).wait_send)
-            pl.when(jnp.logical_and(z2 == z, y > 0))(batch_of(NG - 1, p2_send.at[z2], p1_recv.at[NY]).wait_send)
-
-    @pl.when(shard + 1 < NSHARDS)
-    def _():
-        pass_note.wait_send()
-        pass_codes.wait_send()
+    for row in range(NY):
+        pl.when(jnp.logical_and(y == row, jnp.logical_not(hub)))(
+            batch_of(NY - row, p1_send.at[0], p1_recv.at[0]).wait_send)
+        if row < NY - 1:
+            pl.when(jnp.logical_and(y == row, hub))(batch_of(NY - 1 - row, p1_send.at[0], p1_recv.at[0]).wait_send)
+
+    @pl.when(jnp.logical_and(hub, y > 0))
+    def _():
+        batch_of(NG * NZ - 1, p2_send.at[0], p1_recv.at[0]).wait_send()
+
+    for row in range(NZ):
+        pl.when(jnp.logical_and(hub, jnp.logical_and(y == 0, z == row)))(
+            batch_of(NG * (NZ - 1 - row) + NG - 1, p2_send.at[0], p1_recv.at[0]).wait_send)
 
     @pl.when(shard + 2 < NSHARDS)
     def _():
-        pass_tail.wait_send()
-
-    def hear_column(z2):
-        pltpu.make_async_remote_copy(
-            src_ref=sums.at[0], dst_ref=column.at[z2], send_sem=p2_send.at[z2], recv_sem=p2_recv.at[z2],
-            device_id=(y * NZ + z2, HUB), device_id_type=MESH).wait_recv()
-
-    offset = inside
+        batch_of(4 + 32 + 16, pass_send.at[0], p1_recv.at[0]).wait_send()
+
+    @pl.when(shard + 2 == NSHARDS)
+    def _():
+        batch_of(4 + 32, pass_send.at[0], p1_recv.at[0]).wait_send()
+
+    @pl.when(y > 0)
+    def _():
+        pl.when(hub)(batch_of(NZ - 1, p1_send.at[0], p2_recv.at[0]).wait_recv)
+        pl.when(jnp.logical_not(hub))(batch_of(NZ, p1_send.at[0], p2_recv.at[0]).wait_recv)
+
+    for row in range(NZ):
+        first = jnp.logical_and(y == 0, z == row)
+        pl.when(jnp.logical_and(first, jnp.logical_not(hub)))(
+            batch_of(row + 1, p1_send.at[0], p2_recv.at[0]).wait_recv)
+        if row:
+            pl.when(jnp.logical_and(first, hub))(batch_of(row, p1_send.at[0], p2_recv.at[0]).wait_recv)
+
+    offset = jnp.zeros((1, CODES), F32)
     for z2 in range(NZ):
-        pl.when(jnp.logical_or(feeds(z2), jnp.logical_and(jnp.logical_not(hub), jnp.logical_and(z2 == z, y > 0))))(
-            functools.partial(hear_column, z2))
-    for z2 in range(NZ):
-        offset = offset + jnp.where(jnp.logical_or(z2 < z, y > 0), column[z2], 0.0)
+        offset = offset + jnp.where(jnp.logical_or(z2 <= z, y > 0), column[z2], 0.0)
     off_ref[0:1] = offset - before
     off_ref[1:2] = offset
 
@@ -350,13 +346,15 @@
 def place_kernel(share_ref, gap_ref, inv_ref, off_ref, share_hbm, gap_hbm, buf, sem):
     share = pltpu.make_async_copy(share_ref, share_hbm, sem.at[0])
     share.start()
-    n = LANES
     copies = [share]
-    for i in range(CAP // n):
+    n = CAP // PIECES
+    for i in range(PIECES):
+        for k in range(i * n, (i + 1) * n, LANES):
+            at = pl.ds(k, LANES)
+            offset = off_ref[0:1] if k < HAND else off_ref[1:2]
+            inv = inv_ref[at]
+            buf[at] = gap_ref[at] - jnp.concatenate([inv, inv], axis=1) * offset
         at = pl.ds(i * n, n)
-        inv = inv_ref[at]
-        offset = off_ref[0:1] if i * n < HAND else off_ref[1:2]
-        buf[at] = gap_ref[at] - jnp.concatenate([inv, inv], axis=1) * offset
         copies.append(pltpu.make_async_copy(buf.at[at], gap_hbm.at[at], sem.at[1 + i]))
         copies[-1].start()
     for copy in copies:
@@ -389,13 +387,13 @@
             pltpu.VMEM((8, LANES), jnp.int32),
             pltpu.VMEM((8, LANES), jnp.int32),
             pltpu.VMEM((1, 1, CODES), F32),
-            pltpu.VMEM((PLANE, 1, CODES), F32),
-            pltpu.VMEM((2, 1, CODES), F32),
+            pltpu.VMEM((NZ * NG, 1, CODES), F32),
+            pltpu.VMEM((NG + 2, 1, CODES), F32),
             pltpu.VMEM((NZ, 1, CODES), F32),
             pltpu.VMEM((CODES, 5 * HALF_BLOCKS), BF16),
             pltpu.VMEM((BLOCK, 5 * HALF_BLOCKS), BF16),
             pltpu.SMEM((1,), jnp.int32),
-            dma((2 + ROWS // BLOCK,)), dma((NY,)), dma((NY + 1,)), dma((NZ,)), dma((NZ,)), dma((3,)), dma((3,)),
+            dma((2 + ROWS // BLOCK,)), dma((1,)), dma((NY,)), dma((1,)), dma((1,)), dma((1,)), dma((2,)),
         ],
         compiler_params=pltpu.CompilerParams(
             collective_id=0, has_side_effects=True, vmem_limit_bytes=32 * 2**20),
@@ -406,7 +404,7 @@
         out_shape=(jax.ShapeDtypeStruct((CAP, CODES), F32),) * 2,
         in_specs=[vmem] * 4,
         out_specs=(hbm, hbm),
-        scratch_shapes=[pltpu.VMEM((CAP, CODES), F32), dma((1 + CAP // LANES,))],
+        scratch_shapes=[pltpu.VMEM((CAP, CODES), F32), dma((1 + PIECES,))],
         compiler_params=pltpu.CompilerParams(vmem_limit_bytes=16 * 2**20),
         name="place",
     )(*tallies)

time: 18.7 us -> 18.4 us (0.984)
  Pallas kernels: 17.1 us -> 16.9 us
    pallas_call x1, Pallas kernels: 16.1 us -> 15.9 us  [local(): pl.pallas_call(tally_kernel, out_shape=(jax.ShapeDtypeStruct((CAP, CODES)...]
where the time goes in v5:
time: 18.4 us; the launch traced here: 18.1 us
  Pallas kernels  16.9 us (92%)
  between operations  1.28 us (7%)
    pallas_call x1, Pallas kernels, local(): pl.pallas_call(tally_kernel, out_shape=(jax.ShapeDtypeStruct((CAP, CODES)...  15.9 us
    pallas_call x1, Pallas kernels, local(): pl.pallas_call(place_kernel, out_shape=(jax.ShapeDtypeStruct((CAP, CODES)...  0.99 us

profile of v5, /device:TPU:9, one launch (start us, length us, event | category | flops | bytes accessed | tf_op | source)
XLA Modules:
  0.0 18.1 jit_solution(14726282373811910671)
XLA Ops:
  1.3 15.9 %tally.1 = (f32[512,256]{1,0:T(8,128)S(1)}, f32[512,256]{1,0:T(8,128)S(1)}, f32[512,128]{1,0:T(8,128)S(1)}, f32[8,256]{1,0:T(8,128)S(1)}) custom-call(s32[64,128]{1,0:T(8,128)} %bitcast.2, s32[6,128]{1,0:T(8,128)} %bitcast.3, s32[1]{0:T(128)S(6)} %copy.5.handed_hbm), custom_call_target="tpu_custom_call" | custom-call | tf_op jit(solution)/shard_map/tally/pallas_call | solution.py:373
  17.1 1.0 %place.1 = (f32[512,256]{1,0:T(8,128)}, f32[512,256]{1,0:T(8,128)}) custom-call(f32[512,256]{1,0:T(8,128)S(1)} %get-tuple-element.6.share_ref, f32[512,256]{1,0:T(8,128)S(1)} %get-tuple-element.7.gap_ref, f32[512,128]{1,0:T(8,128)S(1)} %get-tuple-element.8.inv_ref, f32[8,256]{1,0:T(8,128)S(1)} %get-tuple-element.9.off_ref), custom_call_target="tpu_custom_call" | custom-call | tf_op jit(solution)/shard_map/place/pallas_call | solution.py:402

commit v6 on v5

--- a/solution.py
+++ b/solution.py
@@ -92,7 +92,7 @@
     codes_hbm, ends_hbm, handed_hbm,
     share_ref, gap_ref, inv_ref, off_ref,
     own, prev, prior, note, got, mine, plane, sums, column, counts, blocks, scalars,
-    load_sem, p1_send, p1_recv, p2_send, p2_recv, pass_send, pass_recv,
+    load_sem, p1_send, p1_recv, p2_send, p2_recv, pass_send, pass_recv, ready, home,
 ):
     seq, grp = lax.axis_index("seq"), lax.axis_index("grp")
     y, z = lax.div(seq, NZ), lax.rem(seq, NZ)
@@ -115,9 +115,6 @@
     def greet(row, group):
         pl.semaphore_signal(barrier, inc=1, device_id=(row, group), device_id_type=MESH)
 
-    def feeds(z2):
-        return jnp.logical_or(z2 < z, jnp.logical_and(y > 0, z2 != z))
-
     @pl.when(hub)
     def _():
         for y2 in range(NY - 1):
@@ -128,10 +125,14 @@
         for g2 in range(NG):
             if g2 != HUB:
                 greet(seq, g2)
-
-    pl.when(jnp.logical_not(hub))(functools.partial(greet, seq, HUB))
-    for z2 in range(NZ):
-        pl.when(feeds(z2))(functools.partial(greet, y * NZ + z2, HUB))
+        for z2 in range(1, NZ):
+            @pl.when(z2 > z)
+            def _():
+                for g2 in range(NG):
+                    greet(y * NZ + z2, g2)
+
+    for z2 in range(1, NZ):
+        pl.when(jnp.logical_and(y > 0, z2 > z))(functools.partial(greet, y * NZ + z2, HUB))
 
     for back in (1, 2):
         pl.when(shard >= back)(functools.partial(greet, *device_of(shard - back)))
@@ -164,8 +165,11 @@
     mine[0] = total
     plane[spot] = total
 
-    columns = jnp.where(hub, NG * jnp.where(y > 0, NZ - 1, NZ - 1 - z), 0)
-    pl.semaphore_wait(barrier, jnp.where(hub, NG - 1 + NY - 1 - y, NY - y) + columns + jnp.minimum(NSHARDS - 1 - shard, 2))
+    hears = jnp.where(hub, NY - 1 - y + jnp.where(y > 0, NG * z, 0), NY - y)
+    pl.semaphore_wait(barrier, hears + z + jnp.minimum(NSHARDS - 1 - shard, 2))
+
+    def answer(sem, row):
+        pl.semaphore_signal(sem, inc=1, device_id=(row, HUB), device_id_type=MESH)
 
     def spread_to(row, group, batch):
         return pltpu.make_async_remote_copy(
@@ -200,6 +204,10 @@
     def _():
         pass_tail.start()
 
+    for z2 in range(NZ - 1):
+        pl.when(z2 < z)(functools.partial(answer, ready, y * NZ + z2))
+    pl.when(jnp.logical_not(hub))(functools.partial(answer, home, seq))
+
     enter(3, own[0:32])
     enter(4, own[32:64])
 
@@ -207,6 +215,14 @@
         pltpu.make_async_remote_copy(
             src_ref=sums.at[kind], dst_ref=column.at[z], send_sem=p2_send.at[0], recv_sem=p2_recv.at[0],
             device_id=(y * NZ + z2, g2), device_id_type=MESH).start()
+
+    def send_level():
+        pl.semaphore_wait(ready, NG * (NZ - 1 - z))
+        for z2 in range(1, NZ):
+            @pl.when(z2 > z)
+            def _():
+                for g2 in range(NG):
+                    climb(z2, g2, NG)
 
     @pl.when(hub)
     def _():
@@ -230,11 +246,8 @@
             sums[g2] = below
             below = below + plane[y * NG + g2]
         sums[NG] = below
-        for z2 in range(1, NZ):
-            @pl.when(z2 > z)
-            def _():
-                for g2 in range(NG):
-                    climb(z2, g2, NG)
+        pl.semaphore_wait(home, NG - 1)
+        pl.when(jnp.logical_and(y > 0, z < NZ - 1))(send_level)
         for g2 in range(NG):
             if g2 != HUB:
                 climb(z, g2, g2)
@@ -302,6 +315,8 @@
             gap_ref[rows] = jnp.transpose(gap)
             inv_ref[rows] = jnp.transpose(jnp.broadcast_to(inv[:, at], (LANES, LANES)))
 
+    pl.when(jnp.logical_and(hub, jnp.logical_and(y == 0, z < NZ - 1)))(send_level)
+
     for row in range(NY):
         pl.when(jnp.logical_and(y == row, jnp.logical_not(hub)))(
             batch_of(NY - row, p1_send.at[0], p1_recv.at[0]).wait_send)
@@ -394,6 +409,7 @@
             pltpu.VMEM((BLOCK, 5 * HALF_BLOCKS), BF16),
             pltpu.SMEM((1,), jnp.int32),
             dma((2 + ROWS // BLOCK,)), dma((1,)), dma((NY,)), dma((1,)), dma((1,)), dma((1,)), dma((2,)),
+            pltpu.SemaphoreType.REGULAR, pltpu.SemaphoreType.REGULAR,
         ],
         compiler_params=pltpu.CompilerParams(
             collective_id=0, has_side_effects=True, vmem_limit_bytes=32 * 2**20),

time: 18.4 us -> 18.3 us (level)
  no operation moved by 1% of the time
where the time goes in v6:
time: 18.3 us; the launch traced here: 18.2 us
  Pallas kernels  16.9 us (92%)
  between operations  1.28 us (7%)
    pallas_call x1, Pallas kernels, local(): pl.pallas_call(tally_kernel, out_shape=(jax.ShapeDtypeStruct((CAP, CODES)...  15.9 us
    pallas_call x1, Pallas kernels, local(): pl.pallas_call(place_kernel, out_shape=(jax.ShapeDtypeStruct((CAP, CODES)...  0.99 us

profile of v6, /device:TPU:9, one launch (start us, length us, event | category | flops | bytes accessed | tf_op | source)
XLA Modules:
  0.0 18.2 jit_solution(7985280068037182342)
XLA Ops:
  1.3 15.9 %tally.1 = (f32[512,256]{1,0:T(8,128)S(1)}, f32[512,256]{1,0:T(8,128)S(1)}, f32[512,128]{1,0:T(8,128)S(1)}, f32[8,256]{1,0:T(8,128)S(1)}) custom-call(s32[64,128]{1,0:T(8,128)} %bitcast.2, s32[6,128]{1,0:T(8,128)} %bitcast.3, s32[1]{0:T(128)S(6)} %copy.5.handed_hbm), custom_call_target="tpu_custom_call" | custom-call | tf_op jit(solution)/shard_map/tally/pallas_call | solution.py:388
  17.2 1.0 %place.1 = (f32[512,256]{1,0:T(8,128)}, f32[512,256]{1,0:T(8,128)}) custom-call(f32[512,256]{1,0:T(8,128)S(1)} %get-tuple-element.6.share_ref, f32[512,256]{1,0:T(8,128)S(1)} %get-tuple-element.7.gap_ref, f32[512,128]{1,0:T(8,128)S(1)} %get-tuple-element.8.inv_ref, f32[8,256]{1,0:T(8,128)S(1)} %get-tuple-element.9.off_ref), custom_call_target="tpu_custom_call" | custom-call | tf_op jit(solution)/shard_map/place/pallas_call | solution.py:418

commit v7 on v6

--- a/solution.py
+++ b/solution.py
@@ -118,10 +118,11 @@
     @pl.when(hub)
     def _():
         for y2 in range(NY - 1):
-            @pl.when(y2 < y)
+            @pl.when(y2 < y if y2 else y == 1)
             def _():
                 for g2 in range(NG):
                     greet(y2 * NZ + z, g2)
+        pl.when(y > 1)(functools.partial(greet, z, HUB))
         for g2 in range(NG):
             if g2 != HUB:
                 greet(seq, g2)
@@ -165,7 +166,7 @@
     mine[0] = total
     plane[spot] = total
 
-    hears = jnp.where(hub, NY - 1 - y + jnp.where(y > 0, NG * z, 0), NY - y)
+    hears = jnp.where(hub, NY - 1 - y + jnp.where(y > 0, NG * z, 0), jnp.where(y == 0, 2, NY - y))
     pl.semaphore_wait(barrier, hears + z + jnp.minimum(NSHARDS - 1 - shard, 2))
 
     def answer(sem, row):
@@ -183,7 +184,8 @@
 
     to_hubs = [(y2, spread_to(y2 * NZ + z, HUB, y)) for y2 in range(NY)]
     for y2, copy in to_hubs:
-        pl.when(jnp.logical_or(y2 > y, jnp.logical_and(y2 == y, jnp.logical_not(hub))))(copy.start)
+        later = jnp.logical_and(y2 > y, y > 0) if y2 > 1 else y2 > y
+        pl.when(jnp.logical_or(later, jnp.logical_and(y2 == y, jnp.logical_not(hub))))(copy.start)
 
     pass_codes = pltpu.make_async_remote_copy(
         src_ref=own, dst_ref=prev, send_sem=pass_send.at[0], recv_sem=pass_recv.at[0],
@@ -227,8 +229,13 @@
     @pl.when(hub)
     def _():
         sums[NG + 1] = jnp.zeros((1, CODES), F32)
+        @pl.when(y > 1)
+        def _():
+            batch_of(1, p1_send.at[0], p1_recv.at[0]).wait_recv()
+            sums[NG + 1] = plane[0]
+
         for y2 in range(NY - 1):
-            @pl.when(y2 < y)
+            @pl.when(y2 < y if y2 else y == 1)
             def _():
                 batch_of(NG, p1_send.at[0], p1_recv.at[y2]).wait_recv()
                 part = sums[NG + 1]
@@ -246,6 +253,14 @@
             sums[g2] = below
             below = below + plane[y * NG + g2]
         sums[NG] = below
+
+        @pl.when(y == 0)
+        def _():
+            for y2 in (2, 3):
+                pltpu.make_async_remote_copy(
+                    src_ref=sums.at[NG], dst_ref=plane.at[0], send_sem=p1_send.at[0], recv_sem=p1_recv.at[0],
+                    device_id=(y2 * NZ + z, HUB), device_id_type=MESH).start()
+
         pl.semaphore_wait(home, NG - 1)
         pl.when(jnp.logical_and(y > 0, z < NZ - 1))(send_level)
         for g2 in range(NG):
@@ -319,7 +334,7 @@
 
     for row in range(NY):
         pl.when(jnp.logical_and(y == row, jnp.logical_not(hub)))(
-            batch_of(NY - row, p1_send.at[0], p1_recv.at[0]).wait_send)
+            batch_of(NY - row if row else 2, p1_send.at[0], p1_recv.at[0]).wait_send)
         if row < NY - 1:
             pl.when(jnp.logical_and(y == row, hub))(batch_of(NY - 1 - row, p1_send.at[0], p1_recv.at[0]).wait_send)
 

time: 18.3 us -> 18.3 us (level)
  the two profiles are of different devices: /device:TPU:9 before, /device:TPU:17 now
where the time goes in v7:
time: 18.3 us; the launch traced here: 18.2 us
  Pallas kernels  16.9 us (92%)
  between operations  1.28 us (7%)
    pallas_call x1, Pallas kernels, local(): pl.pallas_call(tally_kernel, out_shape=(jax.ShapeDtypeStruct((CAP, CODES)...  15.9 us
    pallas_call x1, Pallas kernels, local(): pl.pallas_call(place_kernel, out_shape=(jax.ShapeDtypeStruct((CAP, CODES)...  0.99 us

profile of v7, /device:TPU:17, one launch (start us, length us, event | category | flops | bytes accessed | tf_op | source)
XLA Modules:
  0.0 18.2 jit_solution(12132787010196433742)
XLA Ops:
  1.3 15.9 %tally.1 = (f32[512,256]{1,0:T(8,128)S(1)}, f32[512,256]{1,0:T(8,128)S(1)}, f32[512,128]{1,0:T(8,128)S(1)}, f32[8,256]{1,0:T(8,128)S(1)}) custom-call(s32[64,128]{1,0:T(8,128)} %bitcast.2, s32[6,128]{1,0:T(8,128)} %bitcast.3, s32[1]{0:T(128)S(6)} %copy.5.handed_hbm), custom_call_target="tpu_custom_call" | custom-call | tf_op jit(solution)/shard_map/tally/pallas_call | solution.py:403
  17.2 1.0 %place.1 = (f32[512,256]{1,0:T(8,128)}, f32[512,256]{1,0:T(8,128)}) custom-call(f32[512,256]{1,0:T(8,128)S(1)} %get-tuple-element.6.share_ref, f32[512,256]{1,0:T(8,128)S(1)} %get-tuple-element.7.gap_ref, f32[512,128]{1,0:T(8,128)S(1)} %get-tuple-element.8.inv_ref, f32[8,256]{1,0:T(8,128)S(1)} %get-tuple-element.9.off_ref), custom_call_target="tpu_custom_call" | custom-call | tf_op jit(solution)/shard_map/place/pallas_call | solution.py:433

commit v8 on v6

--- a/solution.py
+++ b/solution.py
@@ -101,8 +101,8 @@
     hub = grp == HUB
 
     load_codes = [
-        pltpu.make_async_copy(codes_hbm.at[pl.ds(i * BLOCK, BLOCK)], own.at[pl.ds(i * BLOCK, BLOCK)], load_sem.at[2 + i])
-        for i in range(ROWS // BLOCK)]
+        pltpu.make_async_copy(codes_hbm.at[pl.ds(i * 32, 32)], own.at[pl.ds(i * 32, 32)], load_sem.at[2 + i])
+        for i in range(ROWS // 32)]
     load_ends = pltpu.make_async_copy(ends_hbm, note.at[pl.ds(0, 6)], load_sem.at[0])
     load_handed = pltpu.make_async_copy(handed_hbm, scalars, load_sem.at[1])
     for load in load_codes:
@@ -160,7 +160,8 @@
         load.wait()
         if i + 1 == len(load_codes):
             write_note()
-        spread = spread + block_counts(own[i * BLOCK : (i + 1) * BLOCK].astype(F32))
+        for k in range(i * 32, (i + 1) * 32, BLOCK):
+            spread = spread + block_counts(own[k : k + BLOCK].astype(F32))
     total = dot_nt(jnp.ones((8, LANES), BF16), spread)[0:1]
     mine[0] = total
     plane[spot] = total
@@ -408,7 +409,7 @@
             pltpu.VMEM((CODES, 5 * HALF_BLOCKS), BF16),
             pltpu.VMEM((BLOCK, 5 * HALF_BLOCKS), BF16),
             pltpu.SMEM((1,), jnp.int32),
-            dma((2 + ROWS // BLOCK,)), dma((1,)), dma((NY,)), dma((1,)), dma((1,)), dma((1,)), dma((2,)),
+            dma((2 + ROWS // 32,)), dma((1,)), dma((NY,)), dma((1,)), dma((1,)), dma((1,)), dma((2,)),
             pltpu.SemaphoreType.REGULAR, pltpu.SemaphoreType.REGULAR,
         ],
         compiler_params=pltpu.CompilerParams(

time: 18.3 us -> 18.3 us (level)
  no operation moved by 1% of the time
where the time goes in v8:
time: 18.3 us; the launch traced here: 18.1 us
  Pallas kernels  16.8 us (92%)
  between operations  1.28 us (7%)
    pallas_call x1, Pallas kernels, local(): pl.pallas_call(tally_kernel, out_shape=(jax.ShapeDtypeStruct((CAP, CODES)...  15.9 us
    pallas_call x1, Pallas kernels, local(): pl.pallas_call(place_kernel, out_shape=(jax.ShapeDtypeStruct((CAP, CODES)...  0.99 us

profile of v8, /device:TPU:9, one launch (start us, length us, event | category | flops | bytes accessed | tf_op | source)
XLA Modules:
  0.0 18.1 jit_solution(11399393776142500517)
XLA Ops:
  1.3 15.9 %tally.1 = (f32[512,256]{1,0:T(8,128)S(1)}, f32[512,256]{1,0:T(8,128)S(1)}, f32[512,128]{1,0:T(8,128)S(1)}, f32[8,256]{1,0:T(8,128)S(1)}) custom-call(s32[64,128]{1,0:T(8,128)} %bitcast.2, s32[6,128]{1,0:T(8,128)} %bitcast.3, s32[1]{0:T(128)S(6)} %copy.5.handed_hbm), custom_call_target="tpu_custom_call" | custom-call | tf_op jit(solution)/shard_map/tally/pallas_call | solution.py:389
  17.1 1.0 %place.1 = (f32[512,256]{1,0:T(8,128)}, f32[512,256]{1,0:T(8,128)}) custom-call(f32[512,256]{1,0:T(8,128)S(1)} %get-tuple-element.6.share_ref, f32[512,256]{1,0:T(8,128)S(1)} %get-tuple-element.7.gap_ref, f32[512,128]{1,0:T(8,128)S(1)} %get-tuple-element.8.inv_ref, f32[8,256]{1,0:T(8,128)S(1)} %get-tuple-element.9.off_ref), custom_call_target="tpu_custom_call" | custom-call | tf_op jit(solution)/shard_map/place/pallas_call | solution.py:419
